TPU v7x, 256 devices: a whole 4x4x8 slice. The times are simulated.
256 devices in a mesh: lev: 8 (over x, core), lon: 32 (over y, z).
Axes of the slice: x: 4, y: 4, z: 8, core: 2. Of those that a mesh axis runs over, the one named last changes fastest.
Arguments:
- previous: float32 [72, 64, 16384], P('lev', None, 'lon'), may hold values from -4 to 4
- loss_matrix: float32 [72, 64, 64], P('lev'), may hold values from -3 to 10, as said below
- pair_matrix: float32 [72, 64, 64], P('lev'), may hold values from -0.1875 to 0.1875
- diffusivity: float32 [72], P('lev'), may hold values from 200 to 2000
- mixing: float32 [72], P('lev'), may hold values from 0.1 to 1
Outputs:
- concentration: float32 [72, 64, 16384], P('lev', None, 'lon')
- level_variance: float32 [72, 64], P('lev')
Inputs may be any that keep to these rules, and one draw needn't show every extreme that they name: `loss_matrix`: each of the 72 blocks is symmetric and at least 0.05 times the identity in the positive definite order.
All inputs are finite; a program needn't handle non-finite values.
Results may differ from a plain program's by a relative error of at most 0.00045.
Values sent between devices are 32-bit elements; how exact they have to be, the bound alone decides.
A program may use at most 64 MiB of HBM per device.

v0:
```python
import functools

import jax
import jax.numpy as jnp
from jax import lax
from jax.experimental import pallas as pl
from jax.experimental.pallas import tpu as pltpu
from jax.sharding import PartitionSpec as P

ITERS = 2
F32 = jnp.float32
BF16 = jnp.bfloat16
MESH = pl.DeviceIdType.MESH
HIGHEST = lax.Precision.HIGHEST

S = 64
ORDER = (1, 2, 3, 4, 6, 8, 7, 5)
NN = (((1,), (0,)), ((), ()))
NT = (((1,), (1,)), ((), ()))
TN = (((0,), (0,)), ((), ()))


def split(x):
    high = x.astype(BF16)
    return high, (x - high.astype(F32)).astype(BF16)


def dot3(a, b, dims=NN):
    one = lambda x, y: lax.dot_general(x, y, dims, preferred_element_type=F32)
    return one(a[0], b[0]) + (one(a[0], b[1]) + one(a[1], b[0]))


def mm(a, b, dims=NN):
    return dot3(split(a), split(b), dims)


def mm_full(a, b, dims=NN):
    return lax.dot_general(a, b, dims, precision=HIGHEST, preferred_element_type=F32)


def eye(n):
    rows = lax.broadcasted_iota(jnp.int32, (n, n), 0)
    return (rows == lax.broadcasted_iota(jnp.int32, (n, n), 1)).astype(F32)


def spd_inverses(blocks, low, high, doublings):
    centre, radius = 0.5 * (high + low), 0.5 * (high - low)
    units = [eye(block.shape[0]) for block in blocks]
    inverses = [unit * (1.0 / centre) for unit in units]
    residuals = [unit - block * (1.0 / centre) for unit, block in zip(units, blocks)]
    term = centre / radius
    for step in range(doublings):
        twice = 2.0 * term * term - 1.0
        gain, shift = 2.0 * term * term / twice, 1.0 / twice
        last = step == doublings - 1
        for i, unit in enumerate(units):
            n = unit.shape[0]
            rest = split(residuals[i])
            if step == 0:
                inverses[i] = (inverses[i] + residuals[i] * (1.0 / centre)) * gain
                if not last:
                    residuals[i] = gain * dot3(rest, rest) - shift * unit
                continue
            known = split(inverses[i])
            if last:
                inverses[i] = gain * (inverses[i] + dot3(known, rest))
                continue
            both = dot3(tuple(jnp.concatenate(p, axis=0) for p in zip(known, rest)), rest)
            inverses[i] = gain * (inverses[i] + both[:n])
            residuals[i] = gain * both[n:] - shift * unit
        term = twice
    exact = [unit - mm_full(block, inverse) for unit, block, inverse in zip(units, blocks, inverses)]
    return [inverse + mm(inverse, rest) for inverse, rest in zip(inverses, exact)]


def wide(grid):
    return jnp.concatenate([jnp.concatenate(row, axis=1) if len(row) > 1 else row[0] for row in grid], axis=0)


def interior(shunt, links):
    one = eye(S)
    zero = jnp.zeros((S, S), F32)
    diag = [shunt[i] + (links[i] + links[i + 1]) * one for i in range(8)]
    tie = [-links[i + 1] * one for i in range(7)]
    upper = wide([
        [diag[0], tie[0], zero, zero],
        [tie[0], diag[1], tie[1], zero],
        [zero, tie[1], diag[2], tie[2]],
        [zero, zero, tie[2], diag[3]],
    ])
    lower = wide([[diag[5], zero, tie[5]], [zero, diag[7], tie[6]], [tie[5], tie[6], diag[6]]])
    upper_inverse, = spd_inverses([upper], 77.0, 8700.0, 6)
    lower_inverse, = spd_inverses([lower], 117.0, 8700.0, 6)
    upper_t = links[4] * upper_inverse[192:256, :]
    lower_t = links[5] * lower_inverse[0:64, :]
    ground_up = jnp.concatenate([shunt[0] + links[0] * one, shunt[1], shunt[2], shunt[3]], axis=0)
    ground_low = jnp.concatenate([shunt[5], shunt[7] + links[8] * one, shunt[6]], axis=0)
    middle = shunt[4] + mm_full(upper_t, ground_up) + mm_full(lower_t, ground_low)
    middle_inverse, = spd_inverses([middle], 90.0, 4700.0, 5)
    spread = jnp.concatenate([upper_t, lower_t, one], axis=1)
    lifted = mm(middle_inverse, spread)
    return upper_inverse, lower_inverse, spread, lifted


def setup_kernel(link_ref, mix_ref, loss_ref, pair_ref, prev_ref, g_hi, g_lo, hc_hi, hc_lo, hr_hi, hr_lo, pack_ref,
                 pw_hi, pw_lo, pn_hi, pn_lo, field_ref, mixrow_ref, full):
    one = eye(S)
    links = [link_ref[i] for i in range(9)]
    shunt = [loss_ref[i] + one for i in range(9)]
    upper_inverse, lower_inverse, spread, lifted = interior(shunt[1:], links)
    inverse = mm(spread, lifted, TN)
    full[...] = inverse
    full[0:256, 0:256] += upper_inverse
    full[256:448, 256:448] += lower_inverse
    lane = lax.broadcasted_iota(jnp.int32, (512, 128), 1)
    columns = jnp.where(lane < S, links[0] * full[:, 0:128], links[8] * full[:, 256:384])
    hc_hi[...], hc_lo[...] = split(columns)
    rows = jnp.concatenate([links[0] * full[0:64, :], links[8] * full[320:384, :]], axis=0)
    hr_hi[...], hr_lo[...] = split(rows)
    g_hi[...], g_lo[...] = split(full[...])
    stack = jnp.concatenate([shunt[level] for level in ORDER], axis=0)
    ends = mm_full(rows, stack)
    across = links[8] * rows[0:64, 320:384]
    pack_ref[0:64, :] = jnp.concatenate([shunt[0] + ends[0:64], ends[64:128]], axis=1)
    pack_ref[64:96, :] = jnp.concatenate([across[0:32], across[32:64]], axis=1)
    for half in range(2):
        row = lax.broadcasted_iota(jnp.int32, (256, 256), 0) // S
        column = lax.broadcasted_iota(jnp.int32, (256, 256), 1) // S
        tall = jnp.concatenate([pair_ref[level] for level in ORDER[4 * half : 4 * half + 4]], axis=0)
        tall = jnp.concatenate([tall, tall], axis=1)
        tall = jnp.where(row == column, jnp.concatenate([tall, tall], axis=1), 0.0)
        pw_hi[half], pw_lo[half] = split(tall)
    pn_hi[...], pn_lo[...] = split(pair_ref[0])
    for j in range(4):
        both = jnp.concatenate([prev_ref[ORDER[2 * j]], prev_ref[ORDER[2 * j + 1]]], axis=0)
        field_ref[:, 128 * j : 128 * j + 128] = both.T
    last = jnp.concatenate([prev_ref[0], jnp.zeros_like(prev_ref[0])], axis=0)
    field_ref[:, 512:640] = last.T
    lane = lax.broadcasted_iota(jnp.int32, (8, 640), 1) // S
    row = jnp.zeros((8, 640), F32)
    for j, level in enumerate(ORDER + (0,)):
        row = jnp.where(lane == j, mix_ref[level], row)
    mixrow_ref[...] = row


def unpack(packs, q):
    both, folded = packs(q)
    across = jnp.concatenate([folded[:, 0:S], folded[:, S:]], axis=0)
    return both[:, 0:S], both[:, S:], across


def interface_kernel(pack_ref, own_hi, own_lo, msg_hi, msg_lo, rlo_hi, rlo_lo, rhi_hi, rhi_lo, full, wp, wc, rs, rc, own):
    chip = lax.axis_index("lev") // 2
    one = eye(S)
    zero = jnp.zeros((S, S), F32)
    here, below, across = zip(*[
        unpack(lambda q: (pack_ref[q, 0:64, :], pack_ref[q, 64:96, :]), q) for q in range(8)
    ])
    back = [a.T for a in across]
    ground = [here[q] + (below[q - 1] if q else 0.0) for q in range(8)]
    diag = [ground[q] + across[q] + (back[q - 1] if q else 0.0) for q in range(8)]
    upper = wide([
        [diag[0], -across[0], zero, zero],
        [-back[0], diag[1], -across[1], zero],
        [zero, -back[1], diag[2], -across[2]],
        [zero, zero, -back[2], diag[3]],
    ])
    lower = wide([
        [diag[5], -across[5], zero],
        [-back[5], diag[6], -across[6]],
        [zero, -back[6], diag[7]],
    ])
    first = chip < 2
    small = jnp.where(
        first, upper[0:128, 0:128], wide([[1000.0 * one, zero], [zero, diag[7]]])
    )
    upper_inverse, lower_inverse, small_inverse = spd_inverses([upper, lower, small], 9.0, 4700.0, 7)
    upper_t = mm(back[3], upper_inverse[192:256, :])
    lower_t = mm(across[4], lower_inverse[0:64, :])
    middle = (
        ground[4]
        + mm_full(upper_t, jnp.concatenate(ground[0:4], axis=0))
        + mm_full(lower_t, jnp.concatenate([ground[5], ground[6], ground[7] + across[7]], axis=0))
    )
    middle_inverse, = spd_inverses([middle], 9.0, 4700.0, 7)
    spread = jnp.concatenate([upper_t, lower_t, one], axis=1)
    lifted = mm(middle_inverse, spread)
    full[...] = mm(spread, lifted, TN)
    full[0:256, 0:256] += upper_inverse
    full[256:448, 256:448] += lower_inverse
    place = {0: 0, 1: 1, 2: 2, 3: 3, 4: 7, 5: 4, 6: 5, 7: 6}
    link = jnp.where(first, back[1], across[6])
    away = mm(link, small_inverse[64:128, :])

    def block(r, c):
        if r > 7 or c > 7:
            return zero
        r, c = place[r], place[c]
        return full[S * r : S * r + S, S * c : S * c + S]

    def blocks(rows, columns):
        return wide([[block(r, c) for c in columns] for r in rows])

    for c in range(4):
        nodes = (2 * c, 2 * c + 1, 2 * c + 1, 2 * c + 2)

        @pl.when(chip == c)
        def _(c=c, nodes=nodes):
            own[...] = blocks(nodes, nodes)
            wc[...] = blocks(nodes, (4,))
            if c in (0, 3):
                far = [away[:, 0:64], away[:, 64:128]]
                if c == 0:
                    rs[...] = jnp.concatenate([far[0], far[1], far[1], one], axis=1)
                    wp[...] = jnp.concatenate([far[0].T, far[1].T, far[1].T, one], axis=0)
                else:
                    rs[...] = jnp.concatenate([one, far[1], far[1], zero], axis=1)
                    wp[...] = jnp.concatenate([one, far[1].T, far[1].T, zero], axis=0)
            else:
                gate = 2 if c == 1 else 6
                rs[...] = blocks((gate,), nodes)
                wp[...] = blocks(nodes, (gate,))

            def seen(n):
                if n > 7:
                    return zero
                n = place[n]
                return spread[:, S * n : S * n + S]

            rc[...] = jnp.concatenate([seen(n) for n in nodes], axis=1)

    own_hi[...], own_lo[...] = split(own[...])
    none = jnp.zeros((256, S), F32)
    msg = wide([[wp[...], none, wc[...], none], [none, wp[...], none, wc[...]]])
    msg_hi[...], msg_lo[...] = split(msg)
    none = jnp.zeros((S, 256), F32)
    rlo_hi[...], rlo_lo[...] = split(jnp.concatenate([rs[...], none, rc[...], none], axis=0))
    rhi_hi[...], rhi_lo[...] = split(jnp.concatenate([none, rs[...], none, rc[...]], axis=0))


def gather_kernel(pack_ref, all_ref, send_sem, recv_sem, own_sem):
    lev = lax.axis_index("lev")
    barrier = pltpu.get_barrier_semaphore()
    for d in range(1, 8):
        pl.semaphore_signal(barrier, inc=1, device_id={"lev": lax.rem(lev + d, 8)}, device_id_type=MESH)
    keep = pltpu.make_async_copy(pack_ref, all_ref.at[lev], own_sem)
    keep.start()
    pl.semaphore_wait(barrier, 7)
    copies = []
    for d in range(1, 8):
        copy = pltpu.make_async_remote_copy(
            src_ref=pack_ref, dst_ref=all_ref.at[lev], send_sem=send_sem.at[d - 1], recv_sem=recv_sem.at[d - 1],
            device_id={"lev": lax.rem(lev + d, 8)}, device_id_type=MESH,
        )
        copy.start()
        copies.append(copy)
    keep.wait()
    for copy in copies:
        copy.wait()


def solve_kernel(count, field_ref, mixrow_ref, pw_hi, pw_lo, pn_hi, pn_lo, g_hi, g_lo, hc_hi, hc_lo, hr_hi, hr_lo,
                 own_hi, own_lo, msg_hi, msg_lo, rlo_hi, rlo_lo, rhi_hi, rhi_lo,
                 out_ref, var_ref,
                 state, gs_hi, gs_lo, gnode, injs, outgo, incoming, nodes, nodebuf, halo, sums, mysum, sumbuf,
                 halo_send, halo_recv, part_send, part_recv, msg_send, msg_recv, sum_send, sum_recv):
    lev = lax.axis_index("lev")
    lon = lax.axis_index("lon")
    core = lax.rem(lev, 2)
    chip = lev // 2
    partner = lev + 1 - 2 * core
    sibling_chip = chip + 1 - 2 * lax.rem(chip, 2)
    across_base = 2 - 2 * (chip // 2)
    sibling = 2 * sibling_chip + core
    across = [2 * (across_base + i) + core for i in range(2)]
    west, east = lax.rem(lon + count - 1, count), lax.rem(lon + 1, count)

    barrier = pltpu.get_barrier_semaphore()
    for other in [partner, sibling] + across:
        pl.semaphore_signal(barrier, inc=1, device_id={"lev": other}, device_id_type=MESH)

    def greet(d, carry):
        pl.semaphore_signal(barrier, inc=1, device_id={"lon": lax.rem(lon + d, count)}, device_id_type=MESH)
        return carry

    lax.fori_loop(1, count, greet, 0)

    def remote(src, dst, send, recv, where):
        return pltpu.make_async_remote_copy(
            src_ref=src, dst_ref=dst, send_sem=send, recv_sem=recv, device_id=where, device_id_type=MESH
        )

    state[0, 8:520, :] = field_ref[...]
    pl.semaphore_wait(barrier, 3 + count)
    mix_row = mixrow_ref[0:1, :]
    pending = []
    for it in range(ITERS):
        final = it == ITERS - 1
        now = state.at[it]
        first = field_ref.at[0:8] if it == 0 else now.at[8:16]
        last = field_ref.at[504:512] if it == 0 else now.at[512:520]
        to_west = remote(first, halo.at[it, 1], halo_send.at[it, 0], halo_recv.at[it, 1], {"lon": west})
        to_east = remote(last, halo.at[it, 0], halo_send.at[it, 1], halo_recv.at[it, 0], {"lon": east})
        to_west.start()
        to_east.start()
        pending += [to_west, to_east]
        for r in range(0, 512, 128):
            here = state[it, 8 + r : 136 + r, :]
            squares = split(here * here)
            for half in range(2):
                piece = tuple(s[:, 256 * half : 256 * half + 256] for s in squares)
                out = dot3(piece, (pw_hi[half], pw_lo[half]), NT)
                sums[r : r + 128, 256 * half : 256 * half + 256] = out
            piece = tuple(s[:, 512:576] for s in squares)
            sums[r : r + 128, 512:576] = dot3(piece, (pn_hi[...], pn_lo[...]), NT)
        to_west.wait_recv()
        to_east.wait_recv()
        state[it, 0:8, :] = halo[it, 0]
        state[it, 520:528, :] = halo[it, 1]
        for r in range(0, 512, 128):
            here = state[it, 8 + r : 136 + r, 0:576]
            around = state[it, 7 + r : 135 + r, 0:576] + state[it, 9 + r : 137 + r, 0:576]
            forcing = field_ref[r : r + 128, 0:576] - sums[r : r + 128, 0:576] + mix_row[:, 0:576] * (around - 2.0 * here)
            parts = split(forcing[:, 0:512])
            gs_hi[r : r + 128, :], gs_lo[r : r + 128, :] = parts
            node = forcing[:, 512:576]
            push = dot3(parts, (hc_hi[...], hc_lo[...])) + jnp.concatenate([node, jnp.zeros_like(node)], axis=1)
            injs[it, r // 256, r % 256 : r % 256 + 128, :] = push
        give = remote(injs.at[it, 1 - core], gnode.at[it, core], part_send.at[it, 0], part_recv.at[it, 0], {"lev": partner})
        give.start()
        gnode[it, core] = injs[it, core]
        give.wait()
        inj = jnp.concatenate([gnode[it, 0], gnode[it, 1]], axis=1)
        packed = split(jnp.concatenate([inj[0:128], inj[128:256]], axis=1))
        message = dot3(packed, (msg_hi[...], msg_lo[...]))
        outgo[it, 0] = message[:, 0:128]
        outgo[it, 1] = message[:, 128:256]
        sends = [
            remote(outgo.at[it, 1], incoming.at[it, 1 + lax.rem(chip, 2)], msg_send.at[it, 1],
                   msg_recv.at[it, 1 + lax.rem(chip, 2)], {"lev": across[0]}),
            remote(outgo.at[it, 1], incoming.at[it, 1 + lax.rem(chip, 2)], msg_send.at[it, 2],
                   msg_recv.at[it, 1 + lax.rem(chip, 2)], {"lev": across[1]}),
            remote(outgo.at[it, 0], incoming.at[it, 0], msg_send.at[it, 0], msg_recv.at[it, 0], {"lev": sibling}),
        ]
        for send in sends:
            send.start()
        mine = dot3(split(inj), (own_hi[...], own_lo[...]))
        if final:
            for c in range(0, 512, 256):
                parts = (gs_hi[c : c + 256, :], gs_lo[c : c + 256, :])
                for b in range(4):
                    rows = slice(128 * b, 128 * b + 128)
                    value = dot3((g_hi[rows, :], g_lo[rows, :]), parts, NT)
                    for h in range(2):
                        out_ref[ORDER[2 * b + h], :, c : c + 256] = value[64 * h : 64 * h + 64]
        else:
            for r in range(0, 512, 128):
                parts = (gs_hi[r : r + 128, :], gs_lo[r : r + 128, :])
                state[it + 1, 8 + r : 136 + r, 0:512] = dot3(parts, (g_hi[...], g_lo[...]))
        for slot in range(3):
            arrive = remote(outgo.at[it, 0], incoming.at[it, slot], msg_send.at[it, 0], msg_recv.at[it, slot], {"lev": sibling})
            arrive.wait_recv()
        for send in sends:
            send.wait_send()
        heard = split(jnp.concatenate([incoming[it, 0], incoming[it, 1] + incoming[it, 2]], axis=1))
        total = mine + jnp.concatenate(
            [dot3(heard, (rlo_hi[...], rlo_lo[...])), dot3(heard, (rhi_hi[...], rhi_lo[...]))], axis=0
        )
        nodes[it, 0] = total[:, 0:128]
        nodes[it, 1] = total[:, 128:256]
        give = remote(nodes.at[it, 1 - core], nodebuf.at[it, core], part_send.at[it, 1], part_recv.at[it, 1], {"lev": partner})
        give.start()
        nodebuf[it, core] = nodes[it, core]
        give.wait()
        if final:
            for c in range(2):
                ends = nodebuf[it, c]
                parts = split(ends)
                columns = slice(256 * c, 256 * c + 256)
                for b in range(4):
                    rows = slice(128 * b, 128 * b + 128)
                    value = dot3((hc_hi[rows, :], hc_lo[rows, :]), parts, NT)
                    for h in range(2):
                        out_ref[ORDER[2 * b + h], :, columns] += value[64 * h : 64 * h + 64]
                out_ref[0, :, columns] = ends.T[0:64]
        else:
            for c in range(2):
                ends = nodebuf[it, c]
                rows = slice(8 + 256 * c, 264 + 256 * c)
                state[it + 1, rows, 0:512] += dot3(split(ends), (hr_hi[...], hr_lo[...]))
                state[it + 1, rows, 512:640] = jnp.where(
                    lax.broadcasted_iota(jnp.int32, (256, 128), 1) < S, ends, 0.0
                )
    ones = jnp.ones((8, 512), BF16)
    dot1 = lambda x: lax.dot_general(ones, x, NT, preferred_element_type=F32)
    row = lax.broadcasted_iota(jnp.int32, (8, 128), 0)
    packed = jnp.zeros((8, 128), F32)
    for j in range(5):
        pair = [ORDER[2 * j], ORDER[2 * j + 1]] if j < 4 else [0]
        values = [out_ref[level] for level in pair]
        values = jnp.concatenate(values if j < 4 else values + [jnp.zeros_like(values[0])], axis=0)
        high, low = split(values * values)
        packed = jnp.where(row == j, dot1(high) + dot1(low), packed)
    mysum[...] = packed
    sumbuf[lon] = packed
    columns = 512 * count

    def tell(d, carry):
        copy = remote(mysum, sumbuf.at[lon], sum_send.at[d], sum_recv.at[lon], {"lon": lax.rem(lon + d, count)})
        copy.start()
        return carry

    def told(d, carry):
        source = lax.rem(lon + count - d, count)
        copy = remote(mysum, sumbuf.at[source], sum_send.at[d], sum_recv.at[source], {"lon": source})
        copy.wait_recv()
        copy.wait_send()
        return carry

    lax.fori_loop(1, count, tell, 0)
    lax.fori_loop(1, count, told, 0)
    total = jnp.sum(sumbuf[...], axis=0) * (1.0 / columns)
    for j in range(9):
        level = (ORDER + (0,))[j]
        var_ref[level : level + 1, :] = total[j // 2 : j // 2 + 1, S * (j % 2) : S * (j % 2) + S]
    for copy in pending:
        copy.wait_send()


def vmem(count):
    return [pl.BlockSpec(memory_space=pltpu.VMEM)] * count


def two(shape):
    return [jax.ShapeDtypeStruct(shape, BF16)] * 2


def params(**more):
    return pltpu.CompilerParams(vmem_limit_bytes=60 * 2**20, **more)


def local(previous, loss_matrix, pair_matrix, diffusivity, mixing):
    count = lax.axis_size("lon")
    smem = pl.BlockSpec(memory_space=pltpu.SMEM)
    out = pl.pallas_call(
        setup_kernel,
        out_shape=two((512, 512)) + two((512, 128)) + two((128, 512)) + [jax.ShapeDtypeStruct((96, 128), F32)]
        + two((2, 256, 256)) + two((S, S)) + [jax.ShapeDtypeStruct((512, 640), F32), jax.ShapeDtypeStruct((8, 640), F32)],
        in_specs=[smem, smem] + vmem(3),
        out_specs=tuple(vmem(13)),
        scratch_shapes=[pltpu.VMEM((512, 512), F32)],
        compiler_params=params(),
    )(diffusivity, mixing, loss_matrix, pair_matrix, previous)
    g, hc, hr, pack = out[0:2], out[2:4], out[4:6], out[6]
    pairs, field, mixrow = out[7:11], out[11], out[12]
    packs = pl.pallas_call(
        gather_kernel,
        out_shape=jax.ShapeDtypeStruct((8, 96, 128), F32),
        in_specs=vmem(1),
        out_specs=vmem(1)[0],
        scratch_shapes=[pltpu.SemaphoreType.DMA((7,)), pltpu.SemaphoreType.DMA((7,)), pltpu.SemaphoreType.DMA],
        compiler_params=params(collective_id=0, has_side_effects=True),
    )(pack)
    weights = pl.pallas_call(
        interface_kernel,
        out_shape=two((256, 256)) + two((512, 256)) + two((256, 256)) * 2,
        in_specs=vmem(1),
        out_specs=tuple(vmem(8)),
        scratch_shapes=[pltpu.VMEM((512, 512), F32)] + [pltpu.VMEM((256, S), F32)] * 2
        + [pltpu.VMEM((S, 256), F32)] * 2 + [pltpu.VMEM((256, 256), F32)],
        compiler_params=params(),
    )(packs)
    return tuple(pl.pallas_call(
        functools.partial(solve_kernel, count),
        out_shape=[jax.ShapeDtypeStruct((9, S, 512), F32), jax.ShapeDtypeStruct((9, S), F32)],
        in_specs=vmem(20),
        out_specs=tuple(vmem(2)),
        scratch_shapes=[
            pltpu.VMEM((2, 528, 640), F32),
            pltpu.VMEM((512, 512), BF16),
            pltpu.VMEM((512, 512), BF16),
            pltpu.VMEM((2, 2, 256, 128), F32),
            pltpu.VMEM((2, 2, 256, 128), F32),
            pltpu.VMEM((2, 2, 128, 128), F32),
            pltpu.VMEM((2, 3, 128, 128), F32),
            pltpu.VMEM((2, 2, 256, 128), F32),
            pltpu.VMEM((2, 2, 256, 128), F32),
            pltpu.VMEM((2, 2, 8, 640), F32),
            pltpu.VMEM((512, 640), F32),
            pltpu.VMEM((8, 128), F32),
            pltpu.VMEM((count, 8, 128), F32),
            pltpu.SemaphoreType.DMA((2, 2)),
            pltpu.SemaphoreType.DMA((2, 2)),
            pltpu.SemaphoreType.DMA((2, 2)),
            pltpu.SemaphoreType.DMA((2, 2)),
            pltpu.SemaphoreType.DMA((2, 3)),
            pltpu.SemaphoreType.DMA((2, 3)),
            pltpu.SemaphoreType.DMA((count,)),
            pltpu.SemaphoreType.DMA((count,)),
        ],
        compiler_params=params(collective_id=1, has_side_effects=True),
    )(field, mixrow, *pairs, *g, *hc, *hr, *weights))


def solution(mesh):
    placed = (P("lev", None, "lon"), P("lev", None, None), P("lev", None, None), P("lev"), P("lev"))
    return jax.shard_map(
        local,
        mesh=mesh,
        in_specs=placed,
        out_specs=(P("lev", None, "lon"), P("lev", None)),
        check_vma=False,
    )
```

profile of v0, /device:TPU:1, one launch (start us, length us, event | category | flops | bytes accessed | tf_op | source)
XLA Modules:
  0.0 83.1 jit_solution(16913258576033914787)
XLA Ops:
  0.6 11.9 %shard_map.68 = (bf16[512,512]{1,0:T(8,128)(2,1)}, bf16[512,512]{1,0:T(8,128)(2,1)}, bf16[512,128]{1,0:T(8,128)(2,1)}, bf16[512,128]{1,0:T(8,128)(2,1)}, bf16[12...) custom-call(f32[9]{0:T(128)} %link_ref.1, ...), custom_call_target="tpu_custom_call" | custom-call | tf_op jit(solution)/shard_map/pallas_call | solution.py:445
  12.6 12.9 %shard_map.69.pack_ref = f32[8,96,128]{2,1,0:T(8,128)} custom-call(f32[96,128]{1,0:T(8,128)} %get-tuple-element.35.pack_ref), custom_call_target="tpu_custom_call" | custom-call | tf_op jit(solution)/shard_map/pallas_call | solution.py:456
  25.5 9.9 %shard_map.70 = (bf16[256,256]{1,0:T(8,128)(2,1)}, bf16[256,256]{1,0:T(8,128)(2,1)}, bf16[512,256]{1,0:T(8,128)(2,1)}, bf16[512,256]{1,0:T(8,128)(2,1)}, bf16[25...) custom-call(f32[8,96,128]{2,1,0:T(8,128)} %shard_map.69.pack_ref), custom_call_target="tpu_custom_call" | custom-call | tf_op jit(solution)/shard_map/pallas_call | solution.py:464
  35.4 44.7 %shard_map.71 = (f32[9,64,512]{2,1,0:T(8,128)}, f32[9,64]{1,0:T(8,128)}) custom-call(f32[512,640]{1,0:T(8,128)} %get-tuple-element.23.field_ref, f32[8,640]{1,0:T(8,128)} %get-tuple-element.24.mixrow_ref, bf16[2,256,256]{2,1,0:T(8,128)(2,1)} %get-tuple-element.25.pw_hi, bf16[2,256,256]{2,1,0:T(8,128)(2,1)} %get-tuple-element.26.pw_lo, ...), custom_call_target="tpu_custom_call" | custom-call | tf_op jit(solution)/shard_map/pallas_call | solution.py:473
  80.1 0.0 copy-start
  80.2 2.4 %copy.9 = f32[9,64,512]{2,1,0:T(8,128)} copy(f32[9,64,512]{2,1,0:T(8,128)} %get-tuple-element.46) | data formatting | bytes 2359296
  82.5 0.0 copy-done
  82.5 0.6 copy.10
Async XLA Ops:
  80.1 2.4 %copy-start = (f32[9,64]{1,0:T(8,128)S(1)}, f32[9,64]{1,0:T(8,128)}, u32[]{:S(2)}) copy-start(f32[9,64]{1,0:T(8,128)} %get-tuple-element.47) | copy-start | bytes 6916
where the time goes:
time: 83.4 us; the launch traced here: 83.1 us
  Pallas kernels  79.5 us (95%)
  local copies, waits for them, and re-layouts  2.97 us (4%)
    pallas_call x1, Pallas kernels, local(): pl.pallas_call(functools.partial(solve_kernel, count), out_shape=[jax.Sha...  44.7 us
    pallas_call x1, Pallas kernels, local(): pl.pallas_call(gather_kernel, out_shape=jax.ShapeDtypeStruct((8, 96, 128)...  12.9 us
    pallas_call x1, Pallas kernels, local(): pl.pallas_call(setup_kernel, out_shape=two((512, 512)) + two((512, 128))...  11.9 us
    pallas_call x1, Pallas kernels, local(): pl.pallas_call(interface_kernel, out_shape=two((256, 256)) + two((512, 25...  9.91 us
    unnamed x4, local copies, waits for them, and re-layouts  2.97 us

commit v1 on v0

--- a/solution.py
+++ b/solution.py
@@ -102,7 +102,7 @@
     return upper_inverse, lower_inverse, spread, lifted
 
 
-def setup_kernel(link_ref, mix_ref, loss_ref, pair_ref, prev_ref, g_hi, g_lo, hc_hi, hc_lo, hr_hi, hr_lo, pack_ref,
+def setup(link_ref, mix_ref, loss_ref, pair_ref, prev_ref, g_hi, g_lo, hc_hi, hc_lo, hr_hi, hr_lo, pack_ref,
                  pw_hi, pw_lo, pn_hi, pn_lo, field_ref, mixrow_ref, full):
     one = eye(S)
     links = [link_ref[i] for i in range(9)]
@@ -149,7 +149,7 @@
     return both[:, 0:S], both[:, S:], across
 
 
-def interface_kernel(pack_ref, own_hi, own_lo, msg_hi, msg_lo, rlo_hi, rlo_lo, rhi_hi, rhi_lo, full, wp, wc, rs, rc, own):
+def interface(pack_ref, own_hi, own_lo, msg_hi, msg_lo, rlo_hi, rlo_lo, rhi_hi, rhi_lo, full, wp, wc, rs, rc, own):
     chip = lax.axis_index("lev") // 2
     one = eye(S)
     zero = jnp.zeros((S, S), F32)
@@ -238,32 +238,11 @@
     rhi_hi[...], rhi_lo[...] = split(jnp.concatenate([none, rs[...], none, rc[...]], axis=0))
 
 
-def gather_kernel(pack_ref, all_ref, send_sem, recv_sem, own_sem):
-    lev = lax.axis_index("lev")
-    barrier = pltpu.get_barrier_semaphore()
-    for d in range(1, 8):
-        pl.semaphore_signal(barrier, inc=1, device_id={"lev": lax.rem(lev + d, 8)}, device_id_type=MESH)
-    keep = pltpu.make_async_copy(pack_ref, all_ref.at[lev], own_sem)
-    keep.start()
-    pl.semaphore_wait(barrier, 7)
-    copies = []
-    for d in range(1, 8):
-        copy = pltpu.make_async_remote_copy(
-            src_ref=pack_ref, dst_ref=all_ref.at[lev], send_sem=send_sem.at[d - 1], recv_sem=recv_sem.at[d - 1],
-            device_id={"lev": lax.rem(lev + d, 8)}, device_id_type=MESH,
-        )
-        copy.start()
-        copies.append(copy)
-    keep.wait()
-    for copy in copies:
-        copy.wait()
-
-
-def solve_kernel(count, field_ref, mixrow_ref, pw_hi, pw_lo, pn_hi, pn_lo, g_hi, g_lo, hc_hi, hc_lo, hr_hi, hr_lo,
-                 own_hi, own_lo, msg_hi, msg_lo, rlo_hi, rlo_lo, rhi_hi, rhi_lo,
-                 out_ref, var_ref,
-                 state, gs_hi, gs_lo, gnode, injs, outgo, incoming, nodes, nodebuf, halo, sums, mysum, sumbuf,
-                 halo_send, halo_recv, part_send, part_recv, msg_send, msg_recv, sum_send, sum_recv):
+def kernel(count, link_ref, mix_ref, loss_ref, pair_ref, prev_ref, out_ref, var_ref,
+           g_hi, g_lo, hc_hi, hc_lo, hr_hi, hr_lo, pack, pw_hi, pw_lo, pn_hi, pn_lo, field_ref, mixrow_ref, full,
+           packs, own_hi, own_lo, msg_hi, msg_lo, rlo_hi, rlo_lo, rhi_hi, rhi_lo, wp, wc, rs, rc, own,
+           state, gs_hi, gs_lo, gnode, injs, outgo, incoming, nodes, nodebuf, halo, sums, mysum, sumbuf,
+           pack_send, pack_recv, halo_send, halo_recv, part_send, part_recv, msg_send, msg_recv, sum_send, sum_recv):
     lev = lax.axis_index("lev")
     lon = lax.axis_index("lon")
     core = lax.rem(lev, 2)
@@ -272,11 +251,13 @@
     sibling_chip = chip + 1 - 2 * lax.rem(chip, 2)
     across_base = 2 - 2 * (chip // 2)
     sibling = 2 * sibling_chip + core
-    across = [2 * (across_base + i) + core for i in range(2)]
+    far = lax.rem(chip + 2, 4)
+    across = [2 * far + core, 2 * (2 * across_base + 1 - far) + core]
     west, east = lax.rem(lon + count - 1, count), lax.rem(lon + 1, count)
 
     barrier = pltpu.get_barrier_semaphore()
-    for other in [partner, sibling] + across:
+    others = [lax.rem(lev + d, 8) for d in range(1, 8)]
+    for other in others:
         pl.semaphore_signal(barrier, inc=1, device_id={"lev": other}, device_id_type=MESH)
 
     def greet(d, carry):
@@ -290,8 +271,30 @@
             src_ref=src, dst_ref=dst, send_sem=send, recv_sem=recv, device_id=where, device_id_type=MESH
         )
 
+    setup(link_ref, mix_ref, loss_ref, pair_ref, prev_ref, g_hi, g_lo, hc_hi, hc_lo, hr_hi, hr_lo, pack,
+          pw_hi, pw_lo, pn_hi, pn_lo, field_ref, mixrow_ref, full)
+    pl.semaphore_wait(barrier, 6 + count)
+    spread = []
+    for d, other in enumerate(others):
+        copy = remote(pack, packs.at[lev], pack_send.at[d], pack_recv.at[d], {"lev": other})
+        copy.start()
+        spread.append(copy)
+    packs[lev] = pack[...]
     state[0, 8:520, :] = field_ref[...]
-    pl.semaphore_wait(barrier, 3 + count)
+    def product(it):
+        if it == ITERS - 1:
+            for c in range(0, 512, 256):
+                parts = (gs_hi[c : c + 256, :], gs_lo[c : c + 256, :])
+                for b in range(4):
+                    rows = slice(128 * b, 128 * b + 128)
+                    value = dot3((g_hi[rows, :], g_lo[rows, :]), parts, NT)
+                    for h in range(2):
+                        out_ref[ORDER[2 * b + h], :, c : c + 256] = value[64 * h : 64 * h + 64]
+        else:
+            for r in range(0, 512, 128):
+                parts = (gs_hi[r : r + 128, :], gs_lo[r : r + 128, :])
+                state[it + 1, 8 + r : 136 + r, 0:512] = dot3(parts, (g_hi[...], g_lo[...]))
+
     mix_row = mixrow_ref[0:1, :]
     pending = []
     for it in range(ITERS):
@@ -329,6 +332,11 @@
         give = remote(injs.at[it, 1 - core], gnode.at[it, core], part_send.at[it, 0], part_recv.at[it, 0], {"lev": partner})
         give.start()
         gnode[it, core] = injs[it, core]
+        if it == 0:
+            product(it)
+            for copy in spread:
+                copy.wait()
+            interface(packs, own_hi, own_lo, msg_hi, msg_lo, rlo_hi, rlo_lo, rhi_hi, rhi_lo, full, wp, wc, rs, rc, own)
         give.wait()
         inj = jnp.concatenate([gnode[it, 0], gnode[it, 1]], axis=1)
         packed = split(jnp.concatenate([inj[0:128], inj[128:256]], axis=1))
@@ -345,18 +353,8 @@
         for send in sends:
             send.start()
         mine = dot3(split(inj), (own_hi[...], own_lo[...]))
-        if final:
-            for c in range(0, 512, 256):
-                parts = (gs_hi[c : c + 256, :], gs_lo[c : c + 256, :])
-                for b in range(4):
-                    rows = slice(128 * b, 128 * b + 128)
-                    value = dot3((g_hi[rows, :], g_lo[rows, :]), parts, NT)
-                    for h in range(2):
-                        out_ref[ORDER[2 * b + h], :, c : c + 256] = value[64 * h : 64 * h + 64]
-        else:
-            for r in range(0, 512, 128):
-                parts = (gs_hi[r : r + 128, :], gs_lo[r : r + 128, :])
-                state[it + 1, 8 + r : 136 + r, 0:512] = dot3(parts, (g_hi[...], g_lo[...]))
+        if it:
+            product(it)
         for slot in range(3):
             arrive = remote(outgo.at[it, 0], incoming.at[it, slot], msg_send.at[it, 0], msg_recv.at[it, slot], {"lev": sibling})
             arrive.wait_recv()
@@ -431,75 +429,27 @@
     return [pl.BlockSpec(memory_space=pltpu.VMEM)] * count
 
 
-def two(shape):
-    return [jax.ShapeDtypeStruct(shape, BF16)] * 2
-
-
-def params(**more):
-    return pltpu.CompilerParams(vmem_limit_bytes=60 * 2**20, **more)
-
-
 def local(previous, loss_matrix, pair_matrix, diffusivity, mixing):
     count = lax.axis_size("lon")
     smem = pl.BlockSpec(memory_space=pltpu.SMEM)
-    out = pl.pallas_call(
-        setup_kernel,
-        out_shape=two((512, 512)) + two((512, 128)) + two((128, 512)) + [jax.ShapeDtypeStruct((96, 128), F32)]
-        + two((2, 256, 256)) + two((S, S)) + [jax.ShapeDtypeStruct((512, 640), F32), jax.ShapeDtypeStruct((8, 640), F32)],
+    low = lambda *shape: [pltpu.VMEM(shape, BF16)] * 2
+    full = lambda *shape: [pltpu.VMEM(shape, F32)]
+    sems = lambda *shape: [pltpu.SemaphoreType.DMA(shape)] * 2
+    scratch = low(512, 512) + low(512, 128) + low(128, 512) + full(96, 128) + low(2, 256, 256) + low(S, S)
+    scratch += full(512, 640) + full(8, 640) + full(512, 512)
+    scratch += full(8, 96, 128) + low(256, 256) + low(512, 256) + low(256, 256) * 2
+    scratch += full(256, S) * 2 + full(S, 256) * 2 + full(256, 256)
+    scratch += full(2, 528, 640) + low(512, 512) + full(2, 2, 256, 128) * 2 + full(2, 2, 128, 128) + full(2, 3, 128, 128)
+    scratch += full(2, 2, 256, 128) * 2 + full(2, 2, 8, 640) + full(512, 640) + full(8, 128) + full(count, 8, 128)
+    scratch += sems(7) + sems(2, 2) + sems(2, 2) + sems(2, 3) + sems(count)
+    return tuple(pl.pallas_call(
+        functools.partial(kernel, count),
+        out_shape=[jax.ShapeDtypeStruct((9, S, 512), F32), jax.ShapeDtypeStruct((9, S), F32)],
         in_specs=[smem, smem] + vmem(3),
-        out_specs=tuple(vmem(13)),
-        scratch_shapes=[pltpu.VMEM((512, 512), F32)],
-        compiler_params=params(),
-    )(diffusivity, mixing, loss_matrix, pair_matrix, previous)
-    g, hc, hr, pack = out[0:2], out[2:4], out[4:6], out[6]
-    pairs, field, mixrow = out[7:11], out[11], out[12]
-    packs = pl.pallas_call(
-        gather_kernel,
-        out_shape=jax.ShapeDtypeStruct((8, 96, 128), F32),
-        in_specs=vmem(1),
-        out_specs=vmem(1)[0],
-        scratch_shapes=[pltpu.SemaphoreType.DMA((7,)), pltpu.SemaphoreType.DMA((7,)), pltpu.SemaphoreType.DMA],
-        compiler_params=params(collective_id=0, has_side_effects=True),
-    )(pack)
-    weights = pl.pallas_call(
-        interface_kernel,
-        out_shape=two((256, 256)) + two((512, 256)) + two((256, 256)) * 2,
-        in_specs=vmem(1),
-        out_specs=tuple(vmem(8)),
-        scratch_shapes=[pltpu.VMEM((512, 512), F32)] + [pltpu.VMEM((256, S), F32)] * 2
-        + [pltpu.VMEM((S, 256), F32)] * 2 + [pltpu.VMEM((256, 256), F32)],
-        compiler_params=params(),
-    )(packs)
-    return tuple(pl.pallas_call(
-        functools.partial(solve_kernel, count),
-        out_shape=[jax.ShapeDtypeStruct((9, S, 512), F32), jax.ShapeDtypeStruct((9, S), F32)],
-        in_specs=vmem(20),
         out_specs=tuple(vmem(2)),
-        scratch_shapes=[
-            pltpu.VMEM((2, 528, 640), F32),
-            pltpu.VMEM((512, 512), BF16),
-            pltpu.VMEM((512, 512), BF16),
-            pltpu.VMEM((2, 2, 256, 128), F32),
-            pltpu.VMEM((2, 2, 256, 128), F32),
-            pltpu.VMEM((2, 2, 128, 128), F32),
-            pltpu.VMEM((2, 3, 128, 128), F32),
-            pltpu.VMEM((2, 2, 256, 128), F32),
-            pltpu.VMEM((2, 2, 256, 128), F32),
-            pltpu.VMEM((2, 2, 8, 640), F32),
-            pltpu.VMEM((512, 640), F32),
-            pltpu.VMEM((8, 128), F32),
-            pltpu.VMEM((count, 8, 128), F32),
-            pltpu.SemaphoreType.DMA((2, 2)),
-            pltpu.SemaphoreType.DMA((2, 2)),
-            pltpu.SemaphoreType.DMA((2, 2)),
-            pltpu.SemaphoreType.DMA((2, 2)),
-            pltpu.SemaphoreType.DMA((2, 3)),
-            pltpu.SemaphoreType.DMA((2, 3)),
-            pltpu.SemaphoreType.DMA((count,)),
-            pltpu.SemaphoreType.DMA((count,)),
-        ],
-        compiler_params=params(collective_id=1, has_side_effects=True),
-    )(field, mixrow, *pairs, *g, *hc, *hr, *weights))
+        scratch_shapes=scratch,
+        compiler_params=pltpu.CompilerParams(vmem_limit_bytes=60 * 2**20, collective_id=0, has_side_effects=True),
+    )(diffusivity, mixing, loss_matrix, pair_matrix, previous))
 
 
 def solution(mesh):

time: 83.4 us -> 65.1 us (0.78)
  Pallas kernels: 79.5 us -> 61.4 us
    pallas_call x4 -> x1, Pallas kernels: 79.5 us -> 61.4 us  [local(): pl.pallas_call(functools.partial(kernel, count), out_shape=[jax.ShapeDtyp...]
where the time goes in v1:
time: 65.1 us; the launch traced here: 65 us
  Pallas kernels  61.4 us (94%)
  local copies, waits for them, and re-layouts  2.97 us (5%)
    pallas_call x1, Pallas kernels, local(): pl.pallas_call(functools.partial(kernel, count), out_shape=[jax.ShapeDtyp...  61.4 us
    unnamed x4, local copies, waits for them, and re-layouts  2.97 us

profile of v1, /device:TPU:1, one launch (start us, length us, event | category | flops | bytes accessed | tf_op | source)
XLA Modules:
  0.0 65.0 jit_solution(12325057693590596750)
XLA Ops:
  0.6 61.4 %shard_map.68 = (f32[9,64,512]{2,1,0:T(8,128)}, f32[9,64]{1,0:T(8,128)}) custom-call(f32[9]{0:T(128)} %link_ref.1, f32[9]{0:T(128)} %mix_ref.1, f32[9,64,64]{2,1,0:T(8,128)} %loss_ref.1, f32[9,64,64]{2,1,0:T(8,128)} %pair_ref.1, f32[9,64,512]{2,1,0:T(8,128)} %prev_ref.1), custom_call_target="tpu_custom_call" | custom-call | tf_op jit(solution)/shard_map/pallas_call | solution.py:445
  62.0 0.0 copy-start
  62.0 2.4 %copy.9 = f32[9,64,512]{2,1,0:T(8,128)} copy(f32[9,64,512]{2,1,0:T(8,128)} %get-tuple-element.4) | data formatting | bytes 2359296
  64.4 0.0 copy-done
  64.4 0.6 copy.10
Async XLA Ops:
  62.0 2.4 %copy-start = (f32[9,64]{1,0:T(8,128)S(1)}, f32[9,64]{1,0:T(8,128)}, u32[]{:S(2)}) copy-start(f32[9,64]{1,0:T(8,128)} %get-tuple-element.5) | copy-start | bytes 6916

commit v2 on v1

--- a/solution.py
+++ b/solution.py
@@ -14,7 +14,7 @@
 HIGHEST = lax.Precision.HIGHEST
 
 S = 64
-ORDER = (1, 2, 3, 4, 6, 8, 7, 5)
+ORDER = (1, 2, 4, 5, 7, 8, 3, 6)
 NN = (((1,), (0,)), ((), ()))
 NT = (((1,), (1,)), ((), ()))
 TN = (((0,), (0,)), ((), ()))
@@ -43,17 +43,19 @@
     return (rows == lax.broadcasted_iota(jnp.int32, (n, n), 1)).astype(F32)
 
 
-def spd_inverses(blocks, low, high, doublings):
-    centre, radius = 0.5 * (high + low), 0.5 * (high - low)
+def spd_inverses(blocks, lows, high, doublings):
+    centres = [0.5 * (high + low) for low in lows]
     units = [eye(block.shape[0]) for block in blocks]
-    inverses = [unit * (1.0 / centre) for unit in units]
-    residuals = [unit - block * (1.0 / centre) for unit, block in zip(units, blocks)]
-    term = centre / radius
+    inverses = [unit * (1.0 / centre) for unit, centre in zip(units, centres)]
+    residuals = [unit - block * (1.0 / centre) for unit, block, centre in zip(units, blocks, centres)]
+    terms = [(high + low) / (high - low) for low in lows]
     for step in range(doublings):
-        twice = 2.0 * term * term - 1.0
-        gain, shift = 2.0 * term * term / twice, 1.0 / twice
         last = step == doublings - 1
         for i, unit in enumerate(units):
+            twice = 2.0 * terms[i] * terms[i] - 1.0
+            gain, shift = (twice + 1.0) / twice, 1.0 / twice
+            terms[i] = twice
+            centre = centres[i]
             n = unit.shape[0]
             rest = split(residuals[i])
             if step == 0:
@@ -68,61 +70,65 @@
             both = dot3(tuple(jnp.concatenate(p, axis=0) for p in zip(known, rest)), rest)
             inverses[i] = gain * (inverses[i] + both[:n])
             residuals[i] = gain * both[n:] - shift * unit
-        term = twice
     exact = [unit - mm_full(block, inverse) for unit, block, inverse in zip(units, blocks, inverses)]
-    return [inverse + mm(inverse, rest) for inverse, rest in zip(inverses, exact)]
+    step = lambda x, y: lax.dot_general(x.astype(BF16), y.astype(BF16), NN, preferred_element_type=F32)
+    return [inverse + step(inverse, rest) for inverse, rest in zip(inverses, exact)]
 
 
 def wide(grid):
     return jnp.concatenate([jnp.concatenate(row, axis=1) if len(row) > 1 else row[0] for row in grid], axis=0)
 
 
-def interior(shunt, links):
+def interior(link_ref, loss_ref, hr_hi, hr_lo, pack_ref, fill):
     one = eye(S)
     zero = jnp.zeros((S, S), F32)
-    diag = [shunt[i] + (links[i] + links[i + 1]) * one for i in range(8)]
-    tie = [-links[i + 1] * one for i in range(7)]
-    upper = wide([
-        [diag[0], tie[0], zero, zero],
-        [tie[0], diag[1], tie[1], zero],
-        [zero, tie[1], diag[2], tie[2]],
-        [zero, zero, tie[2], diag[3]],
-    ])
-    lower = wide([[diag[5], zero, tie[5]], [zero, diag[7], tie[6]], [tie[5], tie[6], diag[6]]])
-    upper_inverse, = spd_inverses([upper], 77.0, 8700.0, 6)
-    lower_inverse, = spd_inverses([lower], 117.0, 8700.0, 6)
-    upper_t = links[4] * upper_inverse[192:256, :]
-    lower_t = links[5] * lower_inverse[0:64, :]
-    ground_up = jnp.concatenate([shunt[0] + links[0] * one, shunt[1], shunt[2], shunt[3]], axis=0)
-    ground_low = jnp.concatenate([shunt[5], shunt[7] + links[8] * one, shunt[6]], axis=0)
-    middle = shunt[4] + mm_full(upper_t, ground_up) + mm_full(lower_t, ground_low)
-    middle_inverse, = spd_inverses([middle], 90.0, 4700.0, 5)
-    spread = jnp.concatenate([upper_t, lower_t, one], axis=1)
-    lifted = mm(middle_inverse, spread)
-    return upper_inverse, lower_inverse, spread, lifted
-
-
-def setup(link_ref, mix_ref, loss_ref, pair_ref, prev_ref, g_hi, g_lo, hc_hi, hc_lo, hr_hi, hr_lo, pack_ref,
-                 pw_hi, pw_lo, pn_hi, pn_lo, field_ref, mixrow_ref, full):
-    one = eye(S)
     links = [link_ref[i] for i in range(9)]
     shunt = [loss_ref[i] + one for i in range(9)]
-    upper_inverse, lower_inverse, spread, lifted = interior(shunt[1:], links)
-    inverse = mm(spread, lifted, TN)
-    full[...] = inverse
-    full[0:256, 0:256] += upper_inverse
-    full[256:448, 256:448] += lower_inverse
+    blocks = []
+    for top in (1, 4, 7):
+        diag = [shunt[level] + (links[level - 1] + links[level]) * one for level in (top, top + 1)]
+        tie = -links[top] * one
+        blocks.append(wide([[diag[0], tie], [tie, diag[1]]]))
+    pairs = spd_inverses(blocks, [199.0] * 3, 6700.0, 5)
+    none = jnp.zeros((S, 128), F32)
+    spread = wide([
+        [links[2] * pairs[0][S:], links[3] * pairs[1][:S], none],
+        [none, links[5] * pairs[1][S:], links[6] * pairs[2][:S]],
+    ])
+    ground = jnp.concatenate(
+        [shunt[1] + links[0] * one, shunt[2], shunt[4], shunt[5], shunt[7], shunt[8] + links[8] * one], axis=0
+    )
+    own = jnp.concatenate([shunt[3], shunt[6]], axis=0) + mm_full(spread, ground)
+    down = links[5] * spread[0:S, 192:256]
+    up = links[3] * spread[S:, 128:192]
+    fill()
+    middle, = spd_inverses([wide([[own[:S] + down, -down], [-up, own[S:] + up]])], [68.6], 3010.0, 5)
+    spread = jnp.concatenate([spread, eye(128)], axis=1)
+    lifted = mm(middle, spread)
+    lane = lax.broadcasted_iota(jnp.int32, (128, 128), 1)
+    ends = mm(jnp.where(lane < S, spread[:, 0:128], spread[:, 256:384]), lifted, TN)
+    first = jnp.concatenate([ends[0:S, 0:128] + pairs[0][:S], ends[0:S, 128:512]], axis=1)
+    last = jnp.concatenate([ends[S:, 0:256], ends[S:, 256:384] + pairs[2][S:], ends[S:, 384:512]], axis=1)
+    rows = jnp.concatenate([links[0] * first, links[8] * last], axis=0)
+    hr_hi[...], hr_lo[...] = split(rows)
+    loads = mm_full(rows, jnp.concatenate([shunt[level] for level in ORDER], axis=0))
+    across = links[8] * rows[0:S, 320:384]
+    pack_ref[0:64, :] = jnp.concatenate([shunt[0] + loads[0:S], loads[S:]], axis=1)
+    pack_ref[64:96, :] = jnp.concatenate([across[0:32], across[32:64]], axis=1)
+    return pairs, spread, lifted
+
+
+def finish_interior(link_ref, pairs, spread, lifted, g_hi, g_lo, hc_hi, hc_lo, full):
+    full[...] = mm(spread, lifted, TN)
+    for i in range(3):
+        at = slice(128 * i, 128 * i + 128)
+        full[at, at] += pairs[i]
     lane = lax.broadcasted_iota(jnp.int32, (512, 128), 1)
-    columns = jnp.where(lane < S, links[0] * full[:, 0:128], links[8] * full[:, 256:384])
-    hc_hi[...], hc_lo[...] = split(columns)
-    rows = jnp.concatenate([links[0] * full[0:64, :], links[8] * full[320:384, :]], axis=0)
-    hr_hi[...], hr_lo[...] = split(rows)
+    hc_hi[...], hc_lo[...] = split(jnp.where(lane < S, link_ref[0] * full[:, 0:128], link_ref[8] * full[:, 256:384]))
     g_hi[...], g_lo[...] = split(full[...])
-    stack = jnp.concatenate([shunt[level] for level in ORDER], axis=0)
-    ends = mm_full(rows, stack)
-    across = links[8] * rows[0:64, 320:384]
-    pack_ref[0:64, :] = jnp.concatenate([shunt[0] + ends[0:64], ends[64:128]], axis=1)
-    pack_ref[64:96, :] = jnp.concatenate([across[0:32], across[32:64]], axis=1)
+
+
+def pair_weights(pair_ref, pw_hi, pw_lo, pn_hi, pn_lo):
     for half in range(2):
         row = lax.broadcasted_iota(jnp.int32, (256, 256), 0) // S
         column = lax.broadcasted_iota(jnp.int32, (256, 256), 1) // S
@@ -131,11 +137,17 @@
         tall = jnp.where(row == column, jnp.concatenate([tall, tall], axis=1), 0.0)
         pw_hi[half], pw_lo[half] = split(tall)
     pn_hi[...], pn_lo[...] = split(pair_ref[0])
+
+
+def field_of(prev_ref, field_ref):
     for j in range(4):
         both = jnp.concatenate([prev_ref[ORDER[2 * j]], prev_ref[ORDER[2 * j + 1]]], axis=0)
         field_ref[:, 128 * j : 128 * j + 128] = both.T
     last = jnp.concatenate([prev_ref[0], jnp.zeros_like(prev_ref[0])], axis=0)
     field_ref[:, 512:640] = last.T
+
+
+def mix_row_of(mix_ref, mixrow_ref):
     lane = lax.broadcasted_iota(jnp.int32, (8, 640), 1) // S
     row = jnp.zeros((8, 640), F32)
     for j, level in enumerate(ORDER + (0,)):
@@ -172,9 +184,11 @@
     ])
     first = chip < 2
     small = jnp.where(
-        first, upper[0:128, 0:128], wide([[1000.0 * one, zero], [zero, diag[7]]])
+        first, upper[0:128, 0:128], wide([[500.0 * one, zero], [zero, diag[7]]])
     )
-    upper_inverse, lower_inverse, small_inverse = spd_inverses([upper, lower, small], 9.0, 4700.0, 7)
+    upper_inverse, lower_inverse, small_inverse = spd_inverses(
+        [upper, lower, small], [9.6, 21.0, 13.9], 2400.0, 6
+    )
     upper_t = mm(back[3], upper_inverse[192:256, :])
     lower_t = mm(across[4], lower_inverse[0:64, :])
     middle = (
@@ -182,7 +196,7 @@
         + mm_full(upper_t, jnp.concatenate(ground[0:4], axis=0))
         + mm_full(lower_t, jnp.concatenate([ground[5], ground[6], ground[7] + across[7]], axis=0))
     )
-    middle_inverse, = spd_inverses([middle], 9.0, 4700.0, 7)
+    middle_inverse, = spd_inverses([middle], [28.7], 2400.0, 5)
     spread = jnp.concatenate([upper_t, lower_t, one], axis=1)
     lifted = mm(middle_inverse, spread)
     full[...] = mm(spread, lifted, TN)
@@ -238,7 +252,8 @@
     rhi_hi[...], rhi_lo[...] = split(jnp.concatenate([none, rs[...], none, rc[...]], axis=0))
 
 
-def kernel(count, link_ref, mix_ref, loss_ref, pair_ref, prev_ref, out_ref, var_ref,
+def kernel(count, link_hbm, mix_hbm, loss_hbm, pair_hbm, prev_hbm, out_ref, var_ref,
+           link_ref, mix_ref, loss_ref, pair_ref, prev_ref, load_sem,
            g_hi, g_lo, hc_hi, hc_lo, hr_hi, hr_lo, pack, pw_hi, pw_lo, pn_hi, pn_lo, field_ref, mixrow_ref, full,
            packs, own_hi, own_lo, msg_hi, msg_lo, rlo_hi, rlo_lo, rhi_hi, rhi_lo, wp, wc, rs, rc, own,
            state, gs_hi, gs_lo, gnode, injs, outgo, incoming, nodes, nodebuf, halo, sums, mysum, sumbuf,
@@ -255,6 +270,14 @@
     across = [2 * far + core, 2 * (2 * across_base + 1 - far) + core]
     west, east = lax.rem(lon + count - 1, count), lax.rem(lon + 1, count)
 
+    loads = [
+        pltpu.make_async_copy(src, dst, load_sem.at[i])
+        for i, (src, dst) in enumerate([
+            (link_hbm, link_ref), (loss_hbm, loss_ref), (prev_hbm, prev_ref), (pair_hbm, pair_ref), (mix_hbm, mix_ref),
+        ])
+    ]
+    for load in loads:
+        load.start()
     barrier = pltpu.get_barrier_semaphore()
     others = [lax.rem(lev + d, 8) for d in range(1, 8)]
     for other in others:
@@ -271,8 +294,14 @@
             src_ref=src, dst_ref=dst, send_sem=send, recv_sem=recv, device_id=where, device_id_type=MESH
         )
 
-    setup(link_ref, mix_ref, loss_ref, pair_ref, prev_ref, g_hi, g_lo, hc_hi, hc_lo, hr_hi, hr_lo, pack,
-          pw_hi, pw_lo, pn_hi, pn_lo, field_ref, mixrow_ref, full)
+
+    def fill():
+        loads[2].wait()
+        field_of(prev_ref, field_ref)
+
+    loads[0].wait()
+    loads[1].wait()
+    parts = interior(link_ref, loss_ref, hr_hi, hr_lo, pack, fill)
     pl.semaphore_wait(barrier, 6 + count)
     spread = []
     for d, other in enumerate(others):
@@ -295,7 +324,6 @@
                 parts = (gs_hi[r : r + 128, :], gs_lo[r : r + 128, :])
                 state[it + 1, 8 + r : 136 + r, 0:512] = dot3(parts, (g_hi[...], g_lo[...]))
 
-    mix_row = mixrow_ref[0:1, :]
     pending = []
     for it in range(ITERS):
         final = it == ITERS - 1
@@ -307,6 +335,12 @@
         to_west.start()
         to_east.start()
         pending += [to_west, to_east]
+        if it == 0:
+            loads[3].wait()
+            loads[4].wait()
+            mix_row_of(mix_ref, mixrow_ref)
+            pair_weights(pair_ref, pw_hi, pw_lo, pn_hi, pn_lo)
+            finish_interior(link_ref, *parts, g_hi, g_lo, hc_hi, hc_lo, full)
         for r in range(0, 512, 128):
             here = state[it, 8 + r : 136 + r, :]
             squares = split(here * here)
@@ -323,7 +357,7 @@
         for r in range(0, 512, 128):
             here = state[it, 8 + r : 136 + r, 0:576]
             around = state[it, 7 + r : 135 + r, 0:576] + state[it, 9 + r : 137 + r, 0:576]
-            forcing = field_ref[r : r + 128, 0:576] - sums[r : r + 128, 0:576] + mix_row[:, 0:576] * (around - 2.0 * here)
+            forcing = field_ref[r : r + 128, 0:576] - sums[r : r + 128, 0:576] + mixrow_ref[0:1, 0:576] * (around - 2.0 * here)
             parts = split(forcing[:, 0:512])
             gs_hi[r : r + 128, :], gs_lo[r : r + 128, :] = parts
             node = forcing[:, 512:576]
@@ -399,8 +433,8 @@
         values = jnp.concatenate(values if j < 4 else values + [jnp.zeros_like(values[0])], axis=0)
         high, low = split(values * values)
         packed = jnp.where(row == j, dot1(high) + dot1(low), packed)
-    mysum[...] = packed
-    sumbuf[lon] = packed
+    mysum[...] = packed[0:5]
+    sumbuf[lon] = packed[0:5]
     columns = 512 * count
 
     def tell(d, carry):
@@ -425,31 +459,51 @@
         copy.wait_send()
 
 
+def put_out(field_ref, sums_ref, out_ref, var_ref, sem):
+    copies = [
+        pltpu.make_async_copy(field_ref, out_ref, sem.at[0]),
+        pltpu.make_async_copy(sums_ref, var_ref, sem.at[1]),
+    ]
+    for copy in copies:
+        copy.start()
+    for copy in copies:
+        copy.wait()
+
+
 def vmem(count):
     return [pl.BlockSpec(memory_space=pltpu.VMEM)] * count
 
 
 def local(previous, loss_matrix, pair_matrix, diffusivity, mixing):
     count = lax.axis_size("lon")
-    smem = pl.BlockSpec(memory_space=pltpu.SMEM)
     low = lambda *shape: [pltpu.VMEM(shape, BF16)] * 2
     full = lambda *shape: [pltpu.VMEM(shape, F32)]
     sems = lambda *shape: [pltpu.SemaphoreType.DMA(shape)] * 2
-    scratch = low(512, 512) + low(512, 128) + low(128, 512) + full(96, 128) + low(2, 256, 256) + low(S, S)
+    scratch = [pltpu.SMEM((9,), F32)] * 2 + full(9, S, S) * 2 + full(9, S, 512) + [pltpu.SemaphoreType.DMA((5,))] + low(512, 512) + low(512, 128) + low(128, 512) + full(96, 128) + low(2, 256, 256) + low(S, S)
     scratch += full(512, 640) + full(8, 640) + full(512, 512)
     scratch += full(8, 96, 128) + low(256, 256) + low(512, 256) + low(256, 256) * 2
     scratch += full(256, S) * 2 + full(S, 256) * 2 + full(256, 256)
     scratch += full(2, 528, 640) + low(512, 512) + full(2, 2, 256, 128) * 2 + full(2, 2, 128, 128) + full(2, 3, 128, 128)
-    scratch += full(2, 2, 256, 128) * 2 + full(2, 2, 8, 640) + full(512, 640) + full(8, 128) + full(count, 8, 128)
+    scratch += full(2, 2, 256, 128) * 2 + full(2, 2, 8, 640) + full(512, 640) + full(5, 128) + full(count, 5, 128)
     scratch += sems(7) + sems(2, 2) + sems(2, 2) + sems(2, 3) + sems(count)
-    return tuple(pl.pallas_call(
+    shapes = [jax.ShapeDtypeStruct((9, S, 512), F32), jax.ShapeDtypeStruct((9, S), F32)]
+    anywhere = [pl.BlockSpec(memory_space=pl.ANY)] * 2
+    done = pl.pallas_call(
         functools.partial(kernel, count),
-        out_shape=[jax.ShapeDtypeStruct((9, S, 512), F32), jax.ShapeDtypeStruct((9, S), F32)],
-        in_specs=[smem, smem] + vmem(3),
+        out_shape=shapes,
+        in_specs=[pl.BlockSpec(memory_space=pltpu.HBM)] * 5,
         out_specs=tuple(vmem(2)),
         scratch_shapes=scratch,
-        compiler_params=pltpu.CompilerParams(vmem_limit_bytes=60 * 2**20, collective_id=0, has_side_effects=True),
-    )(diffusivity, mixing, loss_matrix, pair_matrix, previous))
+        compiler_params=pltpu.CompilerParams(vmem_limit_bytes=32 * 2**20, collective_id=0, has_side_effects=True),
+    )(*[pltpu.with_memory_space_constraint(x, pltpu.HBM) for x in (diffusivity, mixing, loss_matrix, pair_matrix, previous)])
+    return tuple(pl.pallas_call(
+        put_out,
+        out_shape=shapes,
+        in_specs=vmem(2),
+        out_specs=tuple(anywhere),
+        scratch_shapes=[pltpu.SemaphoreType.DMA((2,))],
+        compiler_params=pltpu.CompilerParams(vmem_limit_bytes=8 * 2**20),
+    )(*done))
 
 
 def solution(mesh):

time: 65.1 us -> 55.1 us (0.85)
  Pallas kernels: 61.4 us -> 54.2 us
  local copies, waits for them, and re-layouts: 2.97 us -> 0 us
    pallas_call x1 -> x2, Pallas kernels: 61.4 us -> 54.2 us  [the longest x1 53.2 us: local(): pl.pallas_call(functools.partial(kernel, count), out_shape=shapes, in_spe...]
    unnamed x4 -> x0, local copies, waits for them, and re-layouts: 2.97 us -> none
where the time goes in v2:
time: 55.1 us; the launch traced here: 55 us
  Pallas kernels  54.2 us (98%)
  between operations  0.8 us (1%)
    pallas_call x1, Pallas kernels, local(): pl.pallas_call(functools.partial(kernel, count), out_shape=shapes, in_spe...  53.2 us

profile of v2, /device:TPU:1, one launch (start us, length us, event | category | flops | bytes accessed | tf_op | source)
XLA Modules:
  0.0 55.0 jit_solution(7471615142211036486)
XLA Ops:
  0.6 53.2 %shard_map.68 = (f32[9,64,512]{2,1,0:T(8,128)S(1)}, f32[9,64]{1,0:T(8,128)S(1)}) custom-call(f32[9]{0:T(128)} %link_hbm.1, f32[9]{0:T(128)} %mix_hbm.1, f32[9,64,64]{2,1,0:T(8,128)} %loss_hbm.1, f32[9,64,64]{2,1,0:T(8,128)} %pair_hbm.1, f32[9,64,512]{2,1,0:T(8,128)} %prev_hbm.1), custom_call_target="tpu_custom_call" | custom-call | tf_op jit(solution)/shard_map/pallas_call | solution.py:491
  53.9 1.0 %shard_map.69 = (f32[9,64,512]{2,1,0:T(8,128)}, f32[9,64]{1,0:T(8,128)}) custom-call(f32[9,64,512]{2,1,0:T(8,128)S(1)} %get-tuple-element.4.field_ref, f32[9,64]{1,0:T(8,128)S(1)} %get-tuple-element.5.sums_ref), custom_call_target="tpu_custom_call" | custom-call | tf_op jit(solution)/shard_map/pallas_call | solution.py:499

commit v3 on v2

--- a/solution.py
+++ b/solution.py
@@ -79,7 +79,7 @@
     return jnp.concatenate([jnp.concatenate(row, axis=1) if len(row) > 1 else row[0] for row in grid], axis=0)
 
 
-def interior(link_ref, loss_ref, hr_hi, hr_lo, pack_ref, fill):
+def interior(link_ref, loss_ref, row_ref, pack_ref, fill):
     one = eye(S)
     zero = jnp.zeros((S, S), F32)
     links = [link_ref[i] for i in range(9)]
@@ -110,7 +110,7 @@
     first = jnp.concatenate([ends[0:S, 0:128] + pairs[0][:S], ends[0:S, 128:512]], axis=1)
     last = jnp.concatenate([ends[S:, 0:256], ends[S:, 256:384] + pairs[2][S:], ends[S:, 384:512]], axis=1)
     rows = jnp.concatenate([links[0] * first, links[8] * last], axis=0)
-    hr_hi[...], hr_lo[...] = split(rows)
+    row_ref[...] = rows
     loads = mm_full(rows, jnp.concatenate([shunt[level] for level in ORDER], axis=0))
     across = links[8] * rows[0:S, 320:384]
     pack_ref[0:64, :] = jnp.concatenate([shunt[0] + loads[0:S], loads[S:]], axis=1)
@@ -118,14 +118,11 @@
     return pairs, spread, lifted
 
 
-def finish_interior(link_ref, pairs, spread, lifted, g_hi, g_lo, hc_hi, hc_lo, full):
+def finish_interior(pairs, spread, lifted, full):
     full[...] = mm(spread, lifted, TN)
     for i in range(3):
         at = slice(128 * i, 128 * i + 128)
         full[at, at] += pairs[i]
-    lane = lax.broadcasted_iota(jnp.int32, (512, 128), 1)
-    hc_hi[...], hc_lo[...] = split(jnp.where(lane < S, link_ref[0] * full[:, 0:128], link_ref[8] * full[:, 256:384]))
-    g_hi[...], g_lo[...] = split(full[...])
 
 
 def pair_weights(pair_ref, pw_hi, pw_lo, pn_hi, pn_lo):
@@ -252,28 +249,28 @@
     rhi_hi[...], rhi_lo[...] = split(jnp.concatenate([none, rs[...], none, rc[...]], axis=0))
 
 
-def kernel(count, link_hbm, mix_hbm, loss_hbm, pair_hbm, prev_hbm, out_ref, var_ref,
+def kernel(count, link_hbm, mix_hbm, loss_hbm, pair_hbm, prev_hbm, out_any, var_ref,
            link_ref, mix_ref, loss_ref, pair_ref, prev_ref, load_sem,
-           g_hi, g_lo, hc_hi, hc_lo, hr_hi, hr_lo, pack, pw_hi, pw_lo, pn_hi, pn_lo, field_ref, mixrow_ref, full,
-           packs, own_hi, own_lo, msg_hi, msg_lo, rlo_hi, rlo_lo, rhi_hi, rhi_lo, wp, wc, rs, rc, own,
-           state, gs_hi, gs_lo, gnode, injs, outgo, incoming, nodes, nodebuf, halo, sums, mysum, sumbuf,
-           pack_send, pack_recv, halo_send, halo_recv, part_send, part_recv, msg_send, msg_recv, sum_send, sum_recv):
+           full, row, g_hi, g_lo, hr_hi, hr_lo, hc_hi, hc_lo, pack, pw_hi, pw_lo, pn_hi, pn_lo, field, mixrow,
+           packs, inverse, own_hi, own_lo, msg_hi, msg_lo, rlo_hi, rlo_lo, rhi_hi, rhi_lo, wp, wc, rs, rc, own,
+           state, gs_hi, gs_lo, injs, outgo, incoming, sums, outs, part, part_in, mysum, sumbuf,
+           pack_send, pack_recv, give_send, give_recv, halo_send, halo_recv, msg_send, msg_recv, out_send, out_recv,
+           sum_send, sum_recv):
     lev = lax.axis_index("lev")
     lon = lax.axis_index("lon")
     core = lax.rem(lev, 2)
     chip = lev // 2
     partner = lev + 1 - 2 * core
-    sibling_chip = chip + 1 - 2 * lax.rem(chip, 2)
+    base = lev - core
+    sibling = 2 * (chip + 1 - 2 * lax.rem(chip, 2)) + core
     across_base = 2 - 2 * (chip // 2)
-    sibling = 2 * sibling_chip + core
     far = lax.rem(chip + 2, 4)
     across = [2 * far + core, 2 * (2 * across_base + 1 - far) + core]
     west, east = lax.rem(lon + count - 1, count), lax.rem(lon + 1, count)
-
     loads = [
         pltpu.make_async_copy(src, dst, load_sem.at[i])
         for i, (src, dst) in enumerate([
-            (link_hbm, link_ref), (loss_hbm, loss_ref), (prev_hbm, prev_ref), (pair_hbm, pair_ref), (mix_hbm, mix_ref),
+            (link_hbm, link_ref), (loss_hbm, loss_ref), (prev_hbm, prev_ref), (pair_hbm, pair_ref.at[core]), (mix_hbm, mix_ref),
         ])
     ]
     for load in loads:
@@ -282,6 +279,8 @@
     others = [lax.rem(lev + d, 8) for d in range(1, 8)]
     for other in others:
         pl.semaphore_signal(barrier, inc=1, device_id={"lev": other}, device_id_type=MESH)
+    for side in (west, east):
+        pl.semaphore_signal(barrier, inc=1, device_id={"lev": partner, "lon": side}, device_id_type=MESH)
 
     def greet(d, carry):
         pl.semaphore_signal(barrier, inc=1, device_id={"lon": lax.rem(lon + d, count)}, device_id_type=MESH)
@@ -294,148 +293,180 @@
             src_ref=src, dst_ref=dst, send_sem=send, recv_sem=recv, device_id=where, device_id_type=MESH
         )
 
+    def rows_at(start, size):
+        return pl.ds(pl.multiple_of(start, 8), size)
+
+    pending = []
+
+    def start(copy):
+        copy.start()
+        pending.append(copy)
+        return copy
 
     def fill():
         loads[2].wait()
-        field_of(prev_ref, field_ref)
+        field_of(prev_ref, field)
 
     loads[0].wait()
     loads[1].wait()
-    parts = interior(link_ref, loss_ref, hr_hi, hr_lo, pack, fill)
-    pl.semaphore_wait(barrier, 6 + count)
+    parts = interior(link_ref, loss_ref, row.at[core], pack, fill)
+    loads[3].wait()
+    loads[4].wait()
+    mix_row_of(mix_ref, mixrow.at[core])
+    pl.semaphore_wait(barrier, 8 + count)
     spread = []
     for d, other in enumerate(others):
         copy = remote(pack, packs.at[lev], pack_send.at[d], pack_recv.at[d], {"lev": other})
         copy.start()
         spread.append(copy)
     packs[lev] = pack[...]
-    state[0, 8:520, :] = field_ref[...]
-    def product(it):
+    away = 1 - core
+    gives = [
+        start(remote(src, dst, give_send.at[i], give_recv.at[i], {"lev": partner}))
+        for i, (src, dst) in enumerate([
+            (field.at[rows_at(248 * away, 264)], state.at[0, core, rows_at(8 * core, 264)]),
+            (pair_ref.at[core], pair_ref.at[core]),
+            (mixrow.at[core], mixrow.at[core]),
+            (row.at[core], row.at[core]),
+        ])
+    ]
+    outer = [
+        start(remote(field.at[0:8], state.at[0, core, 264:272], halo_send.at[0, 0], halo_recv.at[0, core],
+                     {"lev": base + 1, "lon": west})),
+        start(remote(field.at[504:512], state.at[0, core, 0:8], halo_send.at[0, 1], halo_recv.at[0, core],
+                     {"lev": base, "lon": east})),
+    ]
+    state[0, core, rows_at(8 * away, 264), :] = field[rows_at(248 * core, 264), :]
+    finish_interior(*parts, full.at[core])
+    give_full = start(remote(full.at[core], full.at[core], give_send.at[4], give_recv.at[4], {"lev": partner}))
+
+    def pair_term(it, s):
+        for r in range(0, 256, 128):
+            here = state[it, s, 8 + r : 136 + r, :]
+            squares = split(here * here)
+            for half in range(2):
+                piece = tuple(x[:, 256 * half : 256 * half + 256] for x in squares)
+                sums[s, r : r + 128, 256 * half : 256 * half + 256] = dot3(piece, (pw_hi[s, half], pw_lo[s, half]), NT)
+            piece = tuple(x[:, 512:576] for x in squares)
+            sums[s, r : r + 128, 512:576] = dot3(piece, (pn_hi[s], pn_lo[s]), NT)
+
+    def forcing_term(it, s):
+        for r in range(0, 256, 128):
+            here = state[it, s, 8 + r : 136 + r, 0:576]
+            around = state[it, s, 7 + r : 135 + r, 0:576] + state[it, s, 9 + r : 137 + r, 0:576]
+            forcing = state[0, s, 8 + r : 136 + r, 0:576] - sums[s, r : r + 128, 0:576]
+            forcing += mixrow[s, 0:1, 0:576] * (around - 2.0 * here)
+            pieces = split(forcing[:, 0:512])
+            gs_hi[s, r : r + 128, :], gs_lo[s, r : r + 128, :] = pieces
+            node = forcing[:, 512:576]
+            push = dot3(pieces, (hr_hi[s], hr_lo[s]), NT)
+            injs[s, r : r + 128, :] = push + jnp.concatenate([node, jnp.zeros_like(node)], axis=1)
+
+    def weights(s):
+        pair_weights(pair_ref.at[s], pw_hi.at[s], pw_lo.at[s], pn_hi.at[s], pn_lo.at[s])
+        hr_hi[s], hr_lo[s] = split(row[s])
+
+    def product(it, s):
         if it == ITERS - 1:
-            for c in range(0, 512, 256):
-                parts = (gs_hi[c : c + 256, :], gs_lo[c : c + 256, :])
-                for b in range(4):
-                    rows = slice(128 * b, 128 * b + 128)
-                    value = dot3((g_hi[rows, :], g_lo[rows, :]), parts, NT)
-                    for h in range(2):
-                        out_ref[ORDER[2 * b + h], :, c : c + 256] = value[64 * h : 64 * h + 64]
+            for b in range(4):
+                rows = slice(128 * b, 128 * b + 128)
+                value = dot3((g_hi[s, rows, :], g_lo[s, rows, :]), (gs_hi[s], gs_lo[s]), NT)
+                for h in range(2):
+                    outs[s, ORDER[2 * b + h]] = value[64 * h : 64 * h + 64]
         else:
-            for r in range(0, 512, 128):
-                parts = (gs_hi[r : r + 128, :], gs_lo[r : r + 128, :])
-                state[it + 1, 8 + r : 136 + r, 0:512] = dot3(parts, (g_hi[...], g_lo[...]))
-
-    pending = []
+            for r in range(0, 256, 128):
+                pieces = (gs_hi[s, r : r + 128, :], gs_lo[s, r : r + 128, :])
+                state[it + 1, s, 8 + r : 136 + r, 0:512] = dot3(pieces, (g_hi[s], g_lo[s]))
+
+    weights(core)
+    pair_term(0, core)
+    for slot in range(2):
+        pltpu.make_async_copy(field.at[0:8], state.at[0, 0, 0:8], halo_recv.at[0, slot]).wait()
+    forcing_term(0, core)
+    for give in gives:
+        give.wait_recv()
+    weights(away)
+    pair_term(0, away)
+    forcing_term(0, away)
+    for copy in spread:
+        copy.wait()
+    interface(packs, own_hi, own_lo, msg_hi, msg_lo, rlo_hi, rlo_lo, rhi_hi, rhi_lo, inverse, wp, wc, rs, rc, own)
     for it in range(ITERS):
         final = it == ITERS - 1
-        now = state.at[it]
-        first = field_ref.at[0:8] if it == 0 else now.at[8:16]
-        last = field_ref.at[504:512] if it == 0 else now.at[512:520]
-        to_west = remote(first, halo.at[it, 1], halo_send.at[it, 0], halo_recv.at[it, 1], {"lon": west})
-        to_east = remote(last, halo.at[it, 0], halo_send.at[it, 1], halo_recv.at[it, 0], {"lon": east})
-        to_west.start()
-        to_east.start()
-        pending += [to_west, to_east]
-        if it == 0:
-            loads[3].wait()
-            loads[4].wait()
-            mix_row_of(mix_ref, mixrow_ref)
-            pair_weights(pair_ref, pw_hi, pw_lo, pn_hi, pn_lo)
-            finish_interior(link_ref, *parts, g_hi, g_lo, hc_hi, hc_lo, full)
-        for r in range(0, 512, 128):
-            here = state[it, 8 + r : 136 + r, :]
-            squares = split(here * here)
-            for half in range(2):
-                piece = tuple(s[:, 256 * half : 256 * half + 256] for s in squares)
-                out = dot3(piece, (pw_hi[half], pw_lo[half]), NT)
-                sums[r : r + 128, 256 * half : 256 * half + 256] = out
-            piece = tuple(s[:, 512:576] for s in squares)
-            sums[r : r + 128, 512:576] = dot3(piece, (pn_hi[...], pn_lo[...]), NT)
-        to_west.wait_recv()
-        to_east.wait_recv()
-        state[it, 0:8, :] = halo[it, 0]
-        state[it, 520:528, :] = halo[it, 1]
-        for r in range(0, 512, 128):
-            here = state[it, 8 + r : 136 + r, 0:576]
-            around = state[it, 7 + r : 135 + r, 0:576] + state[it, 9 + r : 137 + r, 0:576]
-            forcing = field_ref[r : r + 128, 0:576] - sums[r : r + 128, 0:576] + mixrow_ref[0:1, 0:576] * (around - 2.0 * here)
-            parts = split(forcing[:, 0:512])
-            gs_hi[r : r + 128, :], gs_lo[r : r + 128, :] = parts
-            node = forcing[:, 512:576]
-            push = dot3(parts, (hc_hi[...], hc_lo[...])) + jnp.concatenate([node, jnp.zeros_like(node)], axis=1)
-            injs[it, r // 256, r % 256 : r % 256 + 128, :] = push
-        give = remote(injs.at[it, 1 - core], gnode.at[it, core], part_send.at[it, 0], part_recv.at[it, 0], {"lev": partner})
-        give.start()
-        gnode[it, core] = injs[it, core]
-        if it == 0:
-            product(it)
-            for copy in spread:
-                copy.wait()
-            interface(packs, own_hi, own_lo, msg_hi, msg_lo, rlo_hi, rlo_lo, rhi_hi, rhi_lo, full, wp, wc, rs, rc, own)
-        give.wait()
-        inj = jnp.concatenate([gnode[it, 0], gnode[it, 1]], axis=1)
+        if it:
+            inner_from, inner_to = 8 + 248 * away, 264 * core
+            outer_from, outer_to = 8 + 248 * core, 264 * away
+            halos = [
+                start(remote(state.at[it, :, rows_at(a, 8), :], state.at[it, :, rows_at(b, 8), :],
+                             halo_send.at[it, i], halo_recv.at[it, i], where))
+                for i, (a, b, where) in enumerate([
+                    (outer_from, outer_to, {"lev": partner, "lon": west + (east - west) * core}),
+                    (inner_from, inner_to, {"lev": partner}),
+                ])
+            ]
+            for s in range(2):
+                pair_term(it, s)
+            for halo in halos:
+                halo.wait_recv()
+            for s in range(2):
+                forcing_term(it, s)
+        inj = jnp.concatenate([injs[0], injs[1]], axis=1)
         packed = split(jnp.concatenate([inj[0:128], inj[128:256]], axis=1))
         message = dot3(packed, (msg_hi[...], msg_lo[...]))
         outgo[it, 0] = message[:, 0:128]
         outgo[it, 1] = message[:, 128:256]
-        sends = [
-            remote(outgo.at[it, 1], incoming.at[it, 1 + lax.rem(chip, 2)], msg_send.at[it, 1],
-                   msg_recv.at[it, 1 + lax.rem(chip, 2)], {"lev": across[0]}),
-            remote(outgo.at[it, 1], incoming.at[it, 1 + lax.rem(chip, 2)], msg_send.at[it, 2],
-                   msg_recv.at[it, 1 + lax.rem(chip, 2)], {"lev": across[1]}),
-            remote(outgo.at[it, 0], incoming.at[it, 0], msg_send.at[it, 0], msg_recv.at[it, 0], {"lev": sibling}),
-        ]
-        for send in sends:
-            send.start()
+        slot = 1 + lax.rem(chip, 2)
+        start(remote(outgo.at[it, 1], incoming.at[it, slot], msg_send.at[it, 1], msg_recv.at[it, slot], {"lev": across[0]}))
+        start(remote(outgo.at[it, 1], incoming.at[it, slot], msg_send.at[it, 2], msg_recv.at[it, slot], {"lev": across[1]}))
+        start(remote(outgo.at[it, 0], incoming.at[it, 0], msg_send.at[it, 0], msg_recv.at[it, 0], {"lev": sibling}))
         mine = dot3(split(inj), (own_hi[...], own_lo[...]))
-        if it:
-            product(it)
+        if it == 0:
+            give_full.wait_recv()
+            for s in range(2):
+                g_hi[s], g_lo[s] = split(full[s])
+                hc_hi[s], hc_lo[s] = split(row[s].T)
+        for s in range(2):
+            product(it, s)
         for slot in range(3):
-            arrive = remote(outgo.at[it, 0], incoming.at[it, slot], msg_send.at[it, 0], msg_recv.at[it, slot], {"lev": sibling})
-            arrive.wait_recv()
-        for send in sends:
-            send.wait_send()
+            pltpu.make_async_copy(outgo.at[it, 0], incoming.at[it, slot], msg_recv.at[it, slot]).wait()
         heard = split(jnp.concatenate([incoming[it, 0], incoming[it, 1] + incoming[it, 2]], axis=1))
         total = mine + jnp.concatenate(
             [dot3(heard, (rlo_hi[...], rlo_lo[...])), dot3(heard, (rhi_hi[...], rhi_lo[...]))], axis=0
         )
-        nodes[it, 0] = total[:, 0:128]
-        nodes[it, 1] = total[:, 128:256]
-        give = remote(nodes.at[it, 1 - core], nodebuf.at[it, core], part_send.at[it, 1], part_recv.at[it, 1], {"lev": partner})
-        give.start()
-        nodebuf[it, core] = nodes[it, core]
-        give.wait()
-        if final:
-            for c in range(2):
-                ends = nodebuf[it, c]
-                parts = split(ends)
-                columns = slice(256 * c, 256 * c + 256)
+        for s in range(2):
+            ends = total[:, 128 * s : 128 * s + 128]
+            pieces = split(ends)
+            if final:
                 for b in range(4):
                     rows = slice(128 * b, 128 * b + 128)
-                    value = dot3((hc_hi[rows, :], hc_lo[rows, :]), parts, NT)
+                    value = dot3((hc_hi[s, rows, :], hc_lo[s, rows, :]), pieces, NT)
                     for h in range(2):
-                        out_ref[ORDER[2 * b + h], :, columns] += value[64 * h : 64 * h + 64]
-                out_ref[0, :, columns] = ends.T[0:64]
-        else:
-            for c in range(2):
-                ends = nodebuf[it, c]
-                rows = slice(8 + 256 * c, 264 + 256 * c)
-                state[it + 1, rows, 0:512] += dot3(split(ends), (hr_hi[...], hr_lo[...]))
-                state[it + 1, rows, 512:640] = jnp.where(
+                        outs[s, ORDER[2 * b + h]] += value[64 * h : 64 * h + 64]
+                outs[s, 0] = ends.T[0:64]
+            else:
+                state[it + 1, s, 8:264, 0:512] += dot3(pieces, (hr_hi[s], hr_lo[s]))
+                state[it + 1, s, 8:264, 512:640] = jnp.where(
                     lax.broadcasted_iota(jnp.int32, (256, 128), 1) < S, ends, 0.0
                 )
-    ones = jnp.ones((8, 512), BF16)
+    ones = jnp.ones((8, 256), BF16)
     dot1 = lambda x: lax.dot_general(ones, x, NT, preferred_element_type=F32)
-    row = lax.broadcasted_iota(jnp.int32, (8, 128), 0)
-    packed = jnp.zeros((8, 128), F32)
-    for j in range(5):
-        pair = [ORDER[2 * j], ORDER[2 * j + 1]] if j < 4 else [0]
-        values = [out_ref[level] for level in pair]
-        values = jnp.concatenate(values if j < 4 else values + [jnp.zeros_like(values[0])], axis=0)
-        high, low = split(values * values)
-        packed = jnp.where(row == j, dot1(high) + dot1(low), packed)
-    mysum[...] = packed[0:5]
-    sumbuf[lon] = packed[0:5]
-    columns = 512 * count
+    line = lax.broadcasted_iota(jnp.int32, (8, 128), 0)
+    for s in range(2):
+        packed = jnp.zeros((8, 128), F32)
+        for j in range(5):
+            values = [outs[s, level] for level in ((ORDER + (0,))[2 * j : 2 * j + 2])]
+            values = jnp.concatenate(values if j < 4 else values + [jnp.zeros_like(values[0])], axis=0)
+            high, low = split(values * values)
+            packed = jnp.where(line == j, dot1(high) + dot1(low), packed)
+        part[s] = packed[0:5]
+    give = start(remote(part.at[away], part_in, out_send.at[0], out_recv.at[0], {"lev": partner}))
+    keep = pltpu.make_async_copy(outs.at[core], out_any.at[core], load_sem.at[0])
+    keep.start()
+    back = start(remote(outs.at[away], out_any.at[core], out_send.at[1], out_recv.at[1], {"lev": partner}))
+    give.wait_recv()
+    mine = part[core] + part_in[...]
+    mysum[...] = mine
+    sumbuf[lon] = mine
 
     def tell(d, carry):
         copy = remote(mysum, sumbuf.at[lon], sum_send.at[d], sum_recv.at[lon], {"lon": lax.rem(lon + d, count)})
@@ -451,19 +482,22 @@
 
     lax.fori_loop(1, count, tell, 0)
     lax.fori_loop(1, count, told, 0)
-    total = jnp.sum(sumbuf[...], axis=0) * (1.0 / columns)
+    total = jnp.sum(sumbuf[...], axis=0) * (1.0 / (512 * count))
     for j in range(9):
         level = (ORDER + (0,))[j]
         var_ref[level : level + 1, :] = total[j // 2 : j // 2 + 1, S * (j % 2) : S * (j % 2) + S]
+    keep.wait()
+    back.wait_recv()
     for copy in pending:
         copy.wait_send()
 
 
 def put_out(field_ref, sums_ref, out_ref, var_ref, sem):
     copies = [
-        pltpu.make_async_copy(field_ref, out_ref, sem.at[0]),
-        pltpu.make_async_copy(sums_ref, var_ref, sem.at[1]),
+        pltpu.make_async_copy(field_ref.at[half], out_ref.at[:, :, pl.ds(256 * half, 256)], sem.at[half])
+        for half in range(2)
     ]
+    copies.append(pltpu.make_async_copy(sums_ref, var_ref, sem.at[2]))
     for copy in copies:
         copy.start()
     for copy in copies:
@@ -479,20 +513,22 @@
     low = lambda *shape: [pltpu.VMEM(shape, BF16)] * 2
     full = lambda *shape: [pltpu.VMEM(shape, F32)]
     sems = lambda *shape: [pltpu.SemaphoreType.DMA(shape)] * 2
-    scratch = [pltpu.SMEM((9,), F32)] * 2 + full(9, S, S) * 2 + full(9, S, 512) + [pltpu.SemaphoreType.DMA((5,))] + low(512, 512) + low(512, 128) + low(128, 512) + full(96, 128) + low(2, 256, 256) + low(S, S)
-    scratch += full(512, 640) + full(8, 640) + full(512, 512)
-    scratch += full(8, 96, 128) + low(256, 256) + low(512, 256) + low(256, 256) * 2
+    scratch = [pltpu.SMEM((9,), F32)] * 2 + full(9, S, S) + full(2, 9, S, S) + full(9, S, 512) + [pltpu.SemaphoreType.DMA((5,))]
+    scratch += full(2, 512, 512) + full(2, 128, 512) + low(2, 512, 512) + low(2, 128, 512) + low(2, 512, 128) + full(96, 128)
+    scratch += low(2, 2, 256, 256) + low(2, S, S) + full(512, 640) + full(2, 8, 640)
+    scratch += full(8, 96, 128) + full(512, 512) + low(256, 256) + low(512, 256) + low(256, 256) * 2
     scratch += full(256, S) * 2 + full(S, 256) * 2 + full(256, 256)
-    scratch += full(2, 528, 640) + low(512, 512) + full(2, 2, 256, 128) * 2 + full(2, 2, 128, 128) + full(2, 3, 128, 128)
-    scratch += full(2, 2, 256, 128) * 2 + full(2, 2, 8, 640) + full(512, 640) + full(5, 128) + full(count, 5, 128)
-    scratch += sems(7) + sems(2, 2) + sems(2, 2) + sems(2, 3) + sems(count)
+    scratch += full(2, 2, 272, 640) + low(2, 256, 512) + full(2, 256, 128) + full(2, 2, 128, 128) + full(2, 3, 128, 128)
+    scratch += full(2, 256, 640) + full(2, 9, S, 256) + full(2, 5, 128) + full(5, 128) * 2 + full(count, 5, 128)
+    scratch += sems(7) + sems(5) + sems(2, 2) + sems(2, 3) + sems(2) + sems(count)
     shapes = [jax.ShapeDtypeStruct((9, S, 512), F32), jax.ShapeDtypeStruct((9, S), F32)]
+    halves = jax.ShapeDtypeStruct((2, 9, S, 256), F32)
     anywhere = [pl.BlockSpec(memory_space=pl.ANY)] * 2
     done = pl.pallas_call(
         functools.partial(kernel, count),
-        out_shape=shapes,
+        out_shape=[halves, shapes[1]],
         in_specs=[pl.BlockSpec(memory_space=pltpu.HBM)] * 5,
-        out_specs=tuple(vmem(2)),
+        out_specs=(anywhere[0], vmem(1)[0]),
         scratch_shapes=scratch,
         compiler_params=pltpu.CompilerParams(vmem_limit_bytes=32 * 2**20, collective_id=0, has_side_effects=True),
     )(*[pltpu.with_memory_space_constraint(x, pltpu.HBM) for x in (diffusivity, mixing, loss_matrix, pair_matrix, previous)])
@@ -501,7 +537,7 @@
         out_shape=shapes,
         in_specs=vmem(2),
         out_specs=tuple(anywhere),
-        scratch_shapes=[pltpu.SemaphoreType.DMA((2,))],
+        scratch_shapes=[pltpu.SemaphoreType.DMA((3,))],
         compiler_params=pltpu.CompilerParams(vmem_limit_bytes=8 * 2**20),
     )(*done))
 

time: 55.1 us -> 52.3 us (0.949)
  Pallas kernels: 54.2 us -> 51.4 us
    pallas_call x1, Pallas kernels: 53.2 us -> 50.4 us  [local(): pl.pallas_call(functools.partial(kernel, count), out_shape=[halves, shape...]
where the time goes in v3:
time: 52.3 us; the launch traced here: 52.2 us
  Pallas kernels  51.4 us (98%)
  between operations  0.8 us (2%)
    pallas_call x1, Pallas kernels, local(): pl.pallas_call(functools.partial(kernel, count), out_shape=[halves, shape...  50.4 us

profile of v3, /device:TPU:1, one launch (start us, length us, event | category | flops | bytes accessed | tf_op | source)
XLA Modules:
  0.0 52.2 jit_solution(13229166626117268065)
XLA Ops:
  0.6 50.4 %shard_map.68 = (f32[2,9,64,256]{3,2,1,0:T(8,128)S(1)}, f32[9,64]{1,0:T(8,128)S(1)}) custom-call(f32[9]{0:T(128)} %link_hbm.1, f32[9]{0:T(128)} %mix_hbm.1, f32[9,64,64]{2,1,0:T(8,128)} %loss_hbm.1, f32[9,64,64]{2,1,0:T(8,128)} %pair_hbm.1, f32[9,64,512]{2,1,0:T(8,128)} %prev_hbm.1), custom_call_target="tpu_custom_call" | custom-call | tf_op jit(solution)/shard_map/pallas_call | solution.py:527
  51.0 1.0 %shard_map.69 = (f32[9,64,512]{2,1,0:T(8,128)}, f32[9,64]{1,0:T(8,128)}) custom-call(f32[2,9,64,256]{3,2,1,0:T(8,128)S(1)} %get-tuple-element.4.field_ref, f32[9,64]{1,0:T(8,128)S(1)} %get-tuple-element.5.sums_ref), custom_call_target="tpu_custom_call" | custom-call | tf_op jit(solution)/shard_map/pallas_call | solution.py:535

commit v4 on v3

--- a/solution.py
+++ b/solution.py
@@ -79,7 +79,7 @@
     return jnp.concatenate([jnp.concatenate(row, axis=1) if len(row) > 1 else row[0] for row in grid], axis=0)
 
 
-def interior(link_ref, loss_ref, row_ref, pack_ref, fill):
+def interior(link_ref, loss_ref, row_ref, pack_ref):
     one = eye(S)
     zero = jnp.zeros((S, S), F32)
     links = [link_ref[i] for i in range(9)]
@@ -101,7 +101,6 @@
     own = jnp.concatenate([shunt[3], shunt[6]], axis=0) + mm_full(spread, ground)
     down = links[5] * spread[0:S, 192:256]
     up = links[3] * spread[S:, 128:192]
-    fill()
     middle, = spd_inverses([wide([[own[:S] + down, -down], [-up, own[S:] + up]])], [68.6], 3010.0, 5)
     spread = jnp.concatenate([spread, eye(128)], axis=1)
     lifted = mm(middle, spread)
@@ -158,7 +157,7 @@
     return both[:, 0:S], both[:, S:], across
 
 
-def interface(pack_ref, own_hi, own_lo, msg_hi, msg_lo, rlo_hi, rlo_lo, rhi_hi, rhi_lo, full, wp, wc, rs, rc, own):
+def interface(pack_ref, own_hi, own_lo, msg_hi, msg_lo, rlo_hi, rlo_lo, rhi_hi, rhi_lo, wp, wc, rs, rc, own):
     chip = lax.axis_index("lev") // 2
     one = eye(S)
     zero = jnp.zeros((S, S), F32)
@@ -196,27 +195,36 @@
     middle_inverse, = spd_inverses([middle], [28.7], 2400.0, 5)
     spread = jnp.concatenate([upper_t, lower_t, one], axis=1)
     lifted = mm(middle_inverse, spread)
-    full[...] = mm(spread, lifted, TN)
-    full[0:256, 0:256] += upper_inverse
-    full[256:448, 256:448] += lower_inverse
     place = {0: 0, 1: 1, 2: 2, 3: 3, 4: 7, 5: 4, 6: 5, 7: 6}
     link = jnp.where(first, back[1], across[6])
     away = mm(link, small_inverse[64:128, :])
 
-    def block(r, c):
-        if r > 7 or c > 7:
-            return zero
-        r, c = place[r], place[c]
-        return full[S * r : S * r + S, S * c : S * c + S]
-
-    def blocks(rows, columns):
-        return wide([[block(r, c) for c in columns] for r in rows])
-
     for c in range(4):
         nodes = (2 * c, 2 * c + 1, 2 * c + 1, 2 * c + 2)
 
         @pl.when(chip == c)
         def _(c=c, nodes=nodes):
+            real = [n for n in range(2 * c, 2 * c + 3) if n < 8]
+            against = real if 4 in real else real + [4]
+            part = lambda x, n: x[:, S * place[n] : S * place[n] + S]
+            both = [jnp.concatenate([part(x, n) for n in which], axis=1) for x, which in ((spread, real), (lifted, against))]
+            product = mm(both[0], both[1], TN)
+
+            def block(r, k):
+                if r not in real or k not in against:
+                    return zero
+                i, j = real.index(r), against.index(k)
+                value = product[S * i : S * i + S, S * j : S * j + S]
+                i, j = place[r], place[k]
+                if i < 4 and j < 4:
+                    value += upper_inverse[S * i : S * i + S, S * j : S * j + S]
+                elif 4 <= i < 7 and 4 <= j < 7:
+                    value += lower_inverse[S * (i - 4) : S * (i - 3), S * (j - 4) : S * (j - 3)]
+                return value
+
+            def blocks(rows, columns):
+                return wide([[block(r, k) for k in columns] for r in rows])
+
             own[...] = blocks(nodes, nodes)
             wc[...] = blocks(nodes, (4,))
             if c in (0, 3):
@@ -249,11 +257,11 @@
     rhi_hi[...], rhi_lo[...] = split(jnp.concatenate([none, rs[...], none, rc[...]], axis=0))
 
 
-def kernel(count, link_hbm, mix_hbm, loss_hbm, pair_hbm, prev_hbm, out_any, var_ref,
+def kernel(count, deep, link_hbm, mix_hbm, loss_hbm, pair_hbm, prev_hbm, out_any, sumbuf,
            link_ref, mix_ref, loss_ref, pair_ref, prev_ref, load_sem,
            full, row, g_hi, g_lo, hr_hi, hr_lo, hc_hi, hc_lo, pack, pw_hi, pw_lo, pn_hi, pn_lo, field, mixrow,
-           packs, inverse, own_hi, own_lo, msg_hi, msg_lo, rlo_hi, rlo_lo, rhi_hi, rhi_lo, wp, wc, rs, rc, own,
-           state, gs_hi, gs_lo, injs, outgo, incoming, sums, outs, part, part_in, mysum, sumbuf,
+           packs, own_hi, own_lo, msg_hi, msg_lo, rlo_hi, rlo_lo, rhi_hi, rhi_lo, wp, wc, rs, rc, own,
+           state, gs_hi, gs_lo, injs, outgo, incoming, sums, outs, ends_ref, part, part_in, mysum,
            pack_send, pack_recv, give_send, give_recv, halo_send, halo_recv, msg_send, msg_recv, out_send, out_recv,
            sum_send, sum_recv):
     lev = lax.axis_index("lev")
@@ -303,23 +311,26 @@
         pending.append(copy)
         return copy
 
-    def fill():
-        loads[2].wait()
-        field_of(prev_ref, field)
-
     loads[0].wait()
     loads[1].wait()
-    parts = interior(link_ref, loss_ref, row.at[core], pack, fill)
+    parts = interior(link_ref, loss_ref, row.at[core], pack)
     loads[3].wait()
     loads[4].wait()
     mix_row_of(mix_ref, mixrow.at[core])
     pl.semaphore_wait(barrier, 8 + count)
-    spread = []
-    for d, other in enumerate(others):
-        copy = remote(pack, packs.at[lev], pack_send.at[d], pack_recv.at[d], {"lev": other})
-        copy.start()
-        spread.append(copy)
     packs[lev] = pack[...]
+    spread = [
+        start(remote(pack, packs.at[lev], pack_send.at[i], pack_recv.at[i], {"lev": target}))
+        for i, target in enumerate([2 * lax.rem(chip + d, 4) + core for d in (2, 1, 3)] + [partner])
+    ]
+    loads[2].wait()
+    field_of(prev_ref, field)
+
+    def hand_on(i, d):
+        spread[i].wait_recv()
+        source = 2 * lax.rem(chip + 4 - d, 4) + core
+        return start(remote(packs.at[source], packs.at[source], pack_send.at[4 + i], pack_recv.at[4 + i], {"lev": partner}))
+
     away = 1 - core
     gives = [
         start(remote(src, dst, give_send.at[i], give_recv.at[i], {"lev": partner}))
@@ -350,17 +361,17 @@
             piece = tuple(x[:, 512:576] for x in squares)
             sums[s, r : r + 128, 512:576] = dot3(piece, (pn_hi[s], pn_lo[s]), NT)
 
-    def forcing_term(it, s):
-        for r in range(0, 256, 128):
-            here = state[it, s, 8 + r : 136 + r, 0:576]
-            around = state[it, s, 7 + r : 135 + r, 0:576] + state[it, s, 9 + r : 137 + r, 0:576]
-            forcing = state[0, s, 8 + r : 136 + r, 0:576] - sums[s, r : r + 128, 0:576]
+    def forcing_term(it, s, chunks=((0, 128), (128, 128))):
+        for r, n in chunks:
+            here = state[it, s, 8 + r : 8 + r + n, 0:576]
+            around = state[it, s, 7 + r : 7 + r + n, 0:576] + state[it, s, 9 + r : 9 + r + n, 0:576]
+            forcing = state[0, s, 8 + r : 8 + r + n, 0:576] - sums[s, r : r + n, 0:576]
             forcing += mixrow[s, 0:1, 0:576] * (around - 2.0 * here)
             pieces = split(forcing[:, 0:512])
-            gs_hi[s, r : r + 128, :], gs_lo[s, r : r + 128, :] = pieces
+            gs_hi[s, r : r + n, :], gs_lo[s, r : r + n, :] = pieces
             node = forcing[:, 512:576]
             push = dot3(pieces, (hr_hi[s], hr_lo[s]), NT)
-            injs[s, r : r + 128, :] = push + jnp.concatenate([node, jnp.zeros_like(node)], axis=1)
+            injs[s, r : r + n, :] = push + jnp.concatenate([node, jnp.zeros_like(node)], axis=1)
 
     def weights(s):
         pair_weights(pair_ref.at[s], pw_hi.at[s], pw_lo.at[s], pn_hi.at[s], pn_lo.at[s])
@@ -383,14 +394,16 @@
     for slot in range(2):
         pltpu.make_async_copy(field.at[0:8], state.at[0, 0, 0:8], halo_recv.at[0, slot]).wait()
     forcing_term(0, core)
+    handed = [hand_on(1, 1), hand_on(2, 3)]
     for give in gives:
         give.wait_recv()
     weights(away)
+    handed.append(hand_on(0, 2))
     pair_term(0, away)
     forcing_term(0, away)
-    for copy in spread:
-        copy.wait()
-    interface(packs, own_hi, own_lo, msg_hi, msg_lo, rlo_hi, rlo_lo, rhi_hi, rhi_lo, inverse, wp, wc, rs, rc, own)
+    for copy in [spread[3]] + handed:
+        copy.wait_recv()
+    interface(packs, own_hi, own_lo, msg_hi, msg_lo, rlo_hi, rlo_lo, rhi_hi, rhi_lo, wp, wc, rs, rc, own)
     for it in range(ITERS):
         final = it == ITERS - 1
         if it:
@@ -406,10 +419,12 @@
             ]
             for s in range(2):
                 pair_term(it, s)
+            for s in range(2):
+                forcing_term(it, s, ((16, 112), (128, 112)))
             for halo in halos:
                 halo.wait_recv()
             for s in range(2):
-                forcing_term(it, s)
+                forcing_term(it, s, ((0, 16), (240, 16)))
         inj = jnp.concatenate([injs[0], injs[1]], axis=1)
         packed = split(jnp.concatenate([inj[0:128], inj[128:256]], axis=1))
         message = dot3(packed, (msg_hi[...], msg_lo[...]))
@@ -433,73 +448,76 @@
         total = mine + jnp.concatenate(
             [dot3(heard, (rlo_hi[...], rlo_lo[...])), dot3(heard, (rhi_hi[...], rhi_lo[...]))], axis=0
         )
-        for s in range(2):
-            ends = total[:, 128 * s : 128 * s + 128]
-            pieces = split(ends)
-            if final:
-                for b in range(4):
-                    rows = slice(128 * b, 128 * b + 128)
-                    value = dot3((hc_hi[s, rows, :], hc_lo[s, rows, :]), pieces, NT)
-                    for h in range(2):
-                        outs[s, ORDER[2 * b + h]] += value[64 * h : 64 * h + 64]
-                outs[s, 0] = ends.T[0:64]
-            else:
-                state[it + 1, s, 8:264, 0:512] += dot3(pieces, (hr_hi[s], hr_lo[s]))
+        if not final:
+            for s in range(2):
+                ends = total[:, 128 * s : 128 * s + 128]
+                state[it + 1, s, 8:264, 0:512] += dot3(split(ends), (hr_hi[s], hr_lo[s]))
                 state[it + 1, s, 8:264, 512:640] = jnp.where(
                     lax.broadcasted_iota(jnp.int32, (256, 128), 1) < S, ends, 0.0
                 )
+    ends_ref[0] = total[:, 0:128]
+    ends_ref[1] = total[:, 128:256]
     ones = jnp.ones((8, 256), BF16)
     dot1 = lambda x: lax.dot_general(ones, x, NT, preferred_element_type=F32)
     line = lax.broadcasted_iota(jnp.int32, (8, 128), 0)
-    for s in range(2):
-        packed = jnp.zeros((8, 128), F32)
-        for j in range(5):
-            values = [outs[s, level] for level in ((ORDER + (0,))[2 * j : 2 * j + 2])]
-            values = jnp.concatenate(values if j < 4 else values + [jnp.zeros_like(values[0])], axis=0)
-            high, low = split(values * values)
-            packed = jnp.where(line == j, dot1(high) + dot1(low), packed)
-        part[s] = packed[0:5]
+
+    def finish(s):
+        ends = ends_ref[s]
+        pieces = split(ends)
+        squares = jnp.zeros((8, 128), F32)
+        for b in range(5):
+            if b < 4:
+                rows = slice(128 * b, 128 * b + 128)
+                value = dot3((hc_hi[s, rows, :], hc_lo[s, rows, :]), pieces, NT)
+                value += jnp.concatenate([outs[s, ORDER[2 * b]], outs[s, ORDER[2 * b + 1]]], axis=0)
+                outs[s, ORDER[2 * b]] = value[0:64]
+                outs[s, ORDER[2 * b + 1]] = value[64:128]
+            else:
+                value = jnp.concatenate([ends.T[0:64], jnp.zeros((64, 256), F32)], axis=0)
+                outs[s, 0] = value[0:64]
+            high, low = split(value * value)
+            squares = jnp.where(line == b, dot1(high) + dot1(low), squares)
+        part[s] = squares[0:5]
+
+    finish(away)
     give = start(remote(part.at[away], part_in, out_send.at[0], out_recv.at[0], {"lev": partner}))
+    back = start(remote(outs.at[away], out_any.at[core], out_send.at[1], out_recv.at[1], {"lev": partner}))
+    finish(core)
     keep = pltpu.make_async_copy(outs.at[core], out_any.at[core], load_sem.at[0])
     keep.start()
-    back = start(remote(outs.at[away], out_any.at[core], out_send.at[1], out_recv.at[1], {"lev": partner}))
     give.wait_recv()
-    mine = part[core] + part_in[...]
-    mysum[...] = mine
-    sumbuf[lon] = mine
-
-    def tell(d, carry):
-        copy = remote(mysum, sumbuf.at[lon], sum_send.at[d], sum_recv.at[lon], {"lon": lax.rem(lon + d, count)})
+    mysum[...] = part[core] + part_in[...]
+    own_sum = pltpu.make_async_copy(mysum, sumbuf.at[lon], load_sem.at[1])
+    own_sum.start()
+    steps = [(dy, dz) for dy in range(deep) for dz in range(count // deep) if dy or dz]
+    steps.sort(key=lambda step: -min(step[0], deep - step[0]) - min(step[1], count // deep - step[1]))
+    wide_z = count // deep
+    y, z = lon // wide_z, lax.rem(lon, wide_z)
+    at = lambda dy, dz: lax.rem(y + dy, deep) * wide_z + lax.rem(z + dz, wide_z)
+    for i, (dy, dz) in enumerate(steps):
+        start(remote(mysum, sumbuf.at[lon], sum_send.at[i], sum_recv.at[lon], {"lon": at(dy, dz)}))
+    keep.wait()
+    back.wait_recv()
+    own_sum.wait()
+    for copy in pending:
+        copy.wait_send()
+    for dy, dz in reversed(steps):
+        source = at(deep - dy, wide_z - dz)
+        pltpu.make_async_copy(mysum, sumbuf.at[source], sum_recv.at[source]).wait()
+
+
+def put_out(field_any, sums_ref, out_ref, var_ref, sem):
+    copies = [
+        pltpu.make_async_copy(field_any.at[half], out_ref.at[:, :, pl.ds(256 * half, 256)], sem.at[half])
+        for half in range(2)
+    ]
+    for copy in copies:
         copy.start()
-        return carry
-
-    def told(d, carry):
-        source = lax.rem(lon + count - d, count)
-        copy = remote(mysum, sumbuf.at[source], sum_send.at[d], sum_recv.at[source], {"lon": source})
-        copy.wait_recv()
-        copy.wait_send()
-        return carry
-
-    lax.fori_loop(1, count, tell, 0)
-    lax.fori_loop(1, count, told, 0)
-    total = jnp.sum(sumbuf[...], axis=0) * (1.0 / (512 * count))
+    count = sums_ref.shape[0]
+    total = jnp.sum(sums_ref[...], axis=0) * (1.0 / (512 * count))
     for j in range(9):
         level = (ORDER + (0,))[j]
         var_ref[level : level + 1, :] = total[j // 2 : j // 2 + 1, S * (j % 2) : S * (j % 2) + S]
-    keep.wait()
-    back.wait_recv()
-    for copy in pending:
-        copy.wait_send()
-
-
-def put_out(field_ref, sums_ref, out_ref, var_ref, sem):
-    copies = [
-        pltpu.make_async_copy(field_ref.at[half], out_ref.at[:, :, pl.ds(256 * half, 256)], sem.at[half])
-        for half in range(2)
-    ]
-    copies.append(pltpu.make_async_copy(sums_ref, var_ref, sem.at[2]))
-    for copy in copies:
-        copy.start()
     for copy in copies:
         copy.wait()
 
@@ -516,28 +534,28 @@
     scratch = [pltpu.SMEM((9,), F32)] * 2 + full(9, S, S) + full(2, 9, S, S) + full(9, S, 512) + [pltpu.SemaphoreType.DMA((5,))]
     scratch += full(2, 512, 512) + full(2, 128, 512) + low(2, 512, 512) + low(2, 128, 512) + low(2, 512, 128) + full(96, 128)
     scratch += low(2, 2, 256, 256) + low(2, S, S) + full(512, 640) + full(2, 8, 640)
-    scratch += full(8, 96, 128) + full(512, 512) + low(256, 256) + low(512, 256) + low(256, 256) * 2
+    scratch += full(8, 96, 128) + low(256, 256) + low(512, 256) + low(256, 256) * 2
     scratch += full(256, S) * 2 + full(S, 256) * 2 + full(256, 256)
     scratch += full(2, 2, 272, 640) + low(2, 256, 512) + full(2, 256, 128) + full(2, 2, 128, 128) + full(2, 3, 128, 128)
-    scratch += full(2, 256, 640) + full(2, 9, S, 256) + full(2, 5, 128) + full(5, 128) * 2 + full(count, 5, 128)
+    scratch += full(2, 256, 640) + full(2, 9, S, 256) + full(2, 256, 128) + full(2, 5, 128) + full(5, 128) * 2
     scratch += sems(7) + sems(5) + sems(2, 2) + sems(2, 3) + sems(2) + sems(count)
     shapes = [jax.ShapeDtypeStruct((9, S, 512), F32), jax.ShapeDtypeStruct((9, S), F32)]
     halves = jax.ShapeDtypeStruct((2, 9, S, 256), F32)
     anywhere = [pl.BlockSpec(memory_space=pl.ANY)] * 2
     done = pl.pallas_call(
-        functools.partial(kernel, count),
-        out_shape=[halves, shapes[1]],
+        functools.partial(kernel, count, 4 if count % 4 == 0 else 1),
+        out_shape=[halves, jax.ShapeDtypeStruct((count, 5, 128), F32)],
         in_specs=[pl.BlockSpec(memory_space=pltpu.HBM)] * 5,
-        out_specs=(anywhere[0], vmem(1)[0]),
+        out_specs=tuple(anywhere),
         scratch_shapes=scratch,
         compiler_params=pltpu.CompilerParams(vmem_limit_bytes=32 * 2**20, collective_id=0, has_side_effects=True),
     )(*[pltpu.with_memory_space_constraint(x, pltpu.HBM) for x in (diffusivity, mixing, loss_matrix, pair_matrix, previous)])
     return tuple(pl.pallas_call(
         put_out,
         out_shape=shapes,
-        in_specs=vmem(2),
-        out_specs=tuple(anywhere),
-        scratch_shapes=[pltpu.SemaphoreType.DMA((3,))],
+        in_specs=anywhere[:1] + vmem(1),
+        out_specs=(anywhere[0], vmem(1)[0]),
+        scratch_shapes=[pltpu.SemaphoreType.DMA((2,))],
         compiler_params=pltpu.CompilerParams(vmem_limit_bytes=8 * 2**20),
     )(*done))
 

time: 52.3 us -> 52.3 us (level)
  no operation moved by 1% of the time
where the time goes in v4:
time: 52.3 us; the launch traced here: 52.2 us
  Pallas kernels  51.4 us (98%)
  between operations  0.8 us (2%)
    pallas_call x1, Pallas kernels, local(): pl.pallas_call(functools.partial(kernel, count, 4 if count % 4 == 0 else...  49.8 us
    pallas_call x1, Pallas kernels, local(): pl.pallas_call(put_out, out_shape=shapes, in_specs=anywhere[:1] + vmem(1)...  1.63 us

profile of v4, /device:TPU:1, one launch (start us, length us, event | category | flops | bytes accessed | tf_op | source)
XLA Modules:
  0.0 52.2 jit_solution(16292264780231239798)
XLA Ops:
  0.6 49.8 %shard_map.68 = (f32[2,9,64,256]{3,2,1,0:T(8,128)S(1)}, f32[32,5,128]{2,1,0:T(8,128)S(1)}) custom-call(f32[9]{0:T(128)} %link_hbm.1, f32[9]{0:T(128)} %mix_hbm.1, f32[9,64,64]{2,1,0:T(8,128)} %loss_hbm.1, f32[9,64,64]{2,1,0:T(8,128)} %pair_hbm.1, f32[9,64,512]{2,1,0:T(8,128)} %prev_hbm.1), custom_call_target="tpu_custom_call" | custom-call | tf_op jit(solution)/shard_map/pallas_call | solution.py:545
  50.5 1.6 %shard_map.69 = (f32[9,64,512]{2,1,0:T(8,128)}, f32[9,64]{1,0:T(8,128)}) custom-call(f32[2,9,64,256]{3,2,1,0:T(8,128)S(1)} %get-tuple-element.4.field_any, f32[32,5,128]{2,1,0:T(8,128)S(1)} %get-tuple-element.5.sums_ref), custom_call_target="tpu_custom_call" | custom-call | tf_op jit(solution)/shard_map/pallas_call | solution.py:553

commit v5 on v4

--- a/solution.py
+++ b/solution.py
@@ -257,11 +257,11 @@
     rhi_hi[...], rhi_lo[...] = split(jnp.concatenate([none, rs[...], none, rc[...]], axis=0))
 
 
-def kernel(count, deep, link_hbm, mix_hbm, loss_hbm, pair_hbm, prev_hbm, out_any, sumbuf,
+def kernel(count, deep, link_hbm, mix_hbm, loss_hbm, pair_hbm, prev_hbm, out_any, var_ref,
            link_ref, mix_ref, loss_ref, pair_ref, prev_ref, load_sem,
            full, row, g_hi, g_lo, hr_hi, hr_lo, hc_hi, hc_lo, pack, pw_hi, pw_lo, pn_hi, pn_lo, field, mixrow,
            packs, own_hi, own_lo, msg_hi, msg_lo, rlo_hi, rlo_lo, rhi_hi, rhi_lo, wp, wc, rs, rc, own,
-           state, gs_hi, gs_lo, injs, outgo, incoming, sums, outs, ends_ref, part, part_in, mysum,
+           state, gs_hi, gs_lo, injs, outgo, incoming, sums, outs, part, part_in, mysum, sumbuf,
            pack_send, pack_recv, give_send, give_recv, halo_send, halo_recv, msg_send, msg_recv, out_send, out_recv,
            sum_send, sum_recv):
     lev = lax.axis_index("lev")
@@ -389,42 +389,35 @@
                 pieces = (gs_hi[s, r : r + 128, :], gs_lo[s, r : r + 128, :])
                 state[it + 1, s, 8 + r : 136 + r, 0:512] = dot3(pieces, (g_hi[s], g_lo[s]))
 
+    middle, edges = ((16, 112), (128, 112)), ((0, 16), (240, 16))
     weights(core)
     pair_term(0, core)
-    for slot in range(2):
-        pltpu.make_async_copy(field.at[0:8], state.at[0, 0, 0:8], halo_recv.at[0, slot]).wait()
-    forcing_term(0, core)
-    handed = [hand_on(1, 1), hand_on(2, 3)]
+    forcing_term(0, core, middle)
     for give in gives:
         give.wait_recv()
     weights(away)
+    handed = [hand_on(1, 1), hand_on(2, 3)]
+    pair_term(0, away)
+    forcing_term(0, away, middle)
     handed.append(hand_on(0, 2))
-    pair_term(0, away)
-    forcing_term(0, away)
+    for slot in range(2):
+        pltpu.make_async_copy(field.at[0:8], state.at[0, 0, 0:8], halo_recv.at[0, slot]).wait()
+    for s in range(2):
+        forcing_term(0, s, edges)
     for copy in [spread[3]] + handed:
         copy.wait_recv()
     interface(packs, own_hi, own_lo, msg_hi, msg_lo, rlo_hi, rlo_lo, rhi_hi, rhi_lo, wp, wc, rs, rc, own)
     for it in range(ITERS):
         final = it == ITERS - 1
         if it:
-            inner_from, inner_to = 8 + 248 * away, 264 * core
-            outer_from, outer_to = 8 + 248 * core, 264 * away
-            halos = [
-                start(remote(state.at[it, :, rows_at(a, 8), :], state.at[it, :, rows_at(b, 8), :],
-                             halo_send.at[it, i], halo_recv.at[it, i], where))
-                for i, (a, b, where) in enumerate([
-                    (outer_from, outer_to, {"lev": partner, "lon": west + (east - west) * core}),
-                    (inner_from, inner_to, {"lev": partner}),
-                ])
-            ]
             for s in range(2):
                 pair_term(it, s)
             for s in range(2):
-                forcing_term(it, s, ((16, 112), (128, 112)))
+                forcing_term(it, s, middle)
             for halo in halos:
                 halo.wait_recv()
             for s in range(2):
-                forcing_term(it, s, ((0, 16), (240, 16)))
+                forcing_term(it, s, edges)
         inj = jnp.concatenate([injs[0], injs[1]], axis=1)
         packed = split(jnp.concatenate([inj[0:128], inj[128:256]], axis=1))
         message = dot3(packed, (msg_hi[...], msg_lo[...]))
@@ -448,76 +441,93 @@
         total = mine + jnp.concatenate(
             [dot3(heard, (rlo_hi[...], rlo_lo[...])), dot3(heard, (rhi_hi[...], rhi_lo[...]))], axis=0
         )
+        total_of = [total[:, 128 * s : 128 * s + 128] for s in range(2)]
         if not final:
+            def land(s, low, high):
+                ends = total_of[s][low:high]
+                rows = slice(8 + low, 8 + high)
+                state[it + 1, s, rows, 0:512] += dot3(split(ends), (hr_hi[s], hr_lo[s]))
+                state[it + 1, s, rows, 512:640] = jnp.where(
+                    lax.broadcasted_iota(jnp.int32, (high - low, 128), 1) < S, ends, 0.0
+                )
+
             for s in range(2):
-                ends = total[:, 128 * s : 128 * s + 128]
-                state[it + 1, s, 8:264, 0:512] += dot3(split(ends), (hr_hi[s], hr_lo[s]))
-                state[it + 1, s, 8:264, 512:640] = jnp.where(
-                    lax.broadcasted_iota(jnp.int32, (256, 128), 1) < S, ends, 0.0
-                )
-    ends_ref[0] = total[:, 0:128]
-    ends_ref[1] = total[:, 128:256]
+                land(s, 0, 16)
+                land(s, 240, 256)
+            inner_from, inner_to = 8 + 248 * away, 264 * core
+            outer_from, outer_to = 8 + 248 * core, 264 * away
+            halos = [
+                start(remote(state.at[it + 1, :, rows_at(a, 8), :], state.at[it + 1, :, rows_at(b, 8), :],
+                             halo_send.at[it + 1, i], halo_recv.at[it + 1, i], where))
+                for i, (a, b, where) in enumerate([
+                    (outer_from, outer_to, {"lev": partner, "lon": west + (east - west) * core}),
+                    (inner_from, inner_to, {"lev": partner}),
+                ])
+            ]
+            for s in range(2):
+                land(s, 16, 240)
+            continue
+        for s in range(2):
+            pieces = split(total_of[s])
+            for b in range(4):
+                rows = slice(128 * b, 128 * b + 128)
+                value = dot3((hc_hi[s, rows, :], hc_lo[s, rows, :]), pieces, NT)
+                for h in range(2):
+                    outs[s, ORDER[2 * b + h]] += value[64 * h : 64 * h + 64]
+            outs[s, 0] = total_of[s].T[0:64]
     ones = jnp.ones((8, 256), BF16)
     dot1 = lambda x: lax.dot_general(ones, x, NT, preferred_element_type=F32)
     line = lax.broadcasted_iota(jnp.int32, (8, 128), 0)
 
-    def finish(s):
-        ends = ends_ref[s]
-        pieces = split(ends)
-        squares = jnp.zeros((8, 128), F32)
-        for b in range(5):
-            if b < 4:
-                rows = slice(128 * b, 128 * b + 128)
-                value = dot3((hc_hi[s, rows, :], hc_lo[s, rows, :]), pieces, NT)
-                value += jnp.concatenate([outs[s, ORDER[2 * b]], outs[s, ORDER[2 * b + 1]]], axis=0)
-                outs[s, ORDER[2 * b]] = value[0:64]
-                outs[s, ORDER[2 * b + 1]] = value[64:128]
-            else:
-                value = jnp.concatenate([ends.T[0:64], jnp.zeros((64, 256), F32)], axis=0)
-                outs[s, 0] = value[0:64]
-            high, low = split(value * value)
-            squares = jnp.where(line == b, dot1(high) + dot1(low), squares)
-        part[s] = squares[0:5]
-
-    finish(away)
+    def squares_of(s):
+        packed = jnp.zeros((8, 128), F32)
+        for j in range(5):
+            values = [outs[s, level] for level in ((ORDER + (0,))[2 * j : 2 * j + 2])]
+            values = jnp.concatenate(values if j < 4 else values + [jnp.zeros_like(values[0])], axis=0)
+            high, low = split(values * values)
+            packed = jnp.where(line == j, dot1(high) + dot1(low), packed)
+        part[s] = packed
+
+    squares_of(away)
     give = start(remote(part.at[away], part_in, out_send.at[0], out_recv.at[0], {"lev": partner}))
     back = start(remote(outs.at[away], out_any.at[core], out_send.at[1], out_recv.at[1], {"lev": partner}))
-    finish(core)
     keep = pltpu.make_async_copy(outs.at[core], out_any.at[core], load_sem.at[0])
     keep.start()
+    squares_of(core)
     give.wait_recv()
-    mysum[...] = part[core] + part_in[...]
-    own_sum = pltpu.make_async_copy(mysum, sumbuf.at[lon], load_sem.at[1])
-    own_sum.start()
-    steps = [(dy, dz) for dy in range(deep) for dz in range(count // deep) if dy or dz]
-    steps.sort(key=lambda step: -min(step[0], deep - step[0]) - min(step[1], count // deep - step[1]))
+    mine = part[core] + part_in[...]
+    mysum[...] = mine
     wide_z = count // deep
     y, z = lon // wide_z, lax.rem(lon, wide_z)
-    at = lambda dy, dz: lax.rem(y + dy, deep) * wide_z + lax.rem(z + dz, wide_z)
+    steps = [(dy, dz) for dy in range(deep) for dz in range(wide_z) if dy or dz]
+    steps.sort(key=lambda step: -min(step[0], deep - step[0]) - min(step[1], wide_z - step[1]))
     for i, (dy, dz) in enumerate(steps):
-        start(remote(mysum, sumbuf.at[lon], sum_send.at[i], sum_recv.at[lon], {"lon": at(dy, dz)}))
+        target = lax.rem(y + dy, deep) * wide_z + lax.rem(z + dz, wide_z)
+        slot = lax.rem(count + lon - target - 1, count)
+        remote(mysum, sumbuf.at[slot], sum_send, sum_recv, {"lon": target}).start()
     keep.wait()
     back.wait_recv()
-    own_sum.wait()
     for copy in pending:
         copy.wait_send()
-    for dy, dz in reversed(steps):
-        source = at(deep - dy, wide_z - dz)
-        pltpu.make_async_copy(mysum, sumbuf.at[source], sum_recv.at[source]).wait()
-
-
-def put_out(field_any, sums_ref, out_ref, var_ref, sem):
+    if steps:
+        slots = sumbuf.at[0 : len(steps)]
+        pltpu.make_async_copy(slots, slots, sum_send).wait()
+        pltpu.make_async_copy(slots, slots, sum_recv).wait()
+        mine = mine + jnp.sum(sumbuf[...], axis=0)
+    total = mine * (1.0 / (512 * count))
+    for j in range(9):
+        level = (ORDER + (0,))[j]
+        var_ref[level : level + 1, :] = total[j // 2 : j // 2 + 1, S * (j % 2) : S * (j % 2) + S]
+
+
+def put_out(field_any, sums_any, out_ref, var_ref, sem):
     copies = [
         pltpu.make_async_copy(field_any.at[half], out_ref.at[:, :, pl.ds(256 * half, 256)], sem.at[half])
         for half in range(2)
     ]
+    copies.append(pltpu.make_async_copy(sums_any, var_ref, sem.at[2]))
     for copy in copies:
         copy.start()
-    count = sums_ref.shape[0]
-    total = jnp.sum(sums_ref[...], axis=0) * (1.0 / (512 * count))
-    for j in range(9):
-        level = (ORDER + (0,))[j]
-        var_ref[level : level + 1, :] = total[j // 2 : j // 2 + 1, S * (j % 2) : S * (j % 2) + S]
     for copy in copies:
         copy.wait()
 
@@ -537,25 +547,25 @@
     scratch += full(8, 96, 128) + low(256, 256) + low(512, 256) + low(256, 256) * 2
     scratch += full(256, S) * 2 + full(S, 256) * 2 + full(256, 256)
     scratch += full(2, 2, 272, 640) + low(2, 256, 512) + full(2, 256, 128) + full(2, 2, 128, 128) + full(2, 3, 128, 128)
-    scratch += full(2, 256, 640) + full(2, 9, S, 256) + full(2, 256, 128) + full(2, 5, 128) + full(5, 128) * 2
-    scratch += sems(7) + sems(5) + sems(2, 2) + sems(2, 3) + sems(2) + sems(count)
+    scratch += full(2, 256, 640) + full(2, 9, S, 256) + full(2, 8, 128) + full(8, 128) * 2 + full(max(count - 1, 1), 8, 128)
+    scratch += sems(7) + sems(5) + sems(2, 2) + sems(2, 3) + sems(2) + [pltpu.SemaphoreType.DMA] * 2
     shapes = [jax.ShapeDtypeStruct((9, S, 512), F32), jax.ShapeDtypeStruct((9, S), F32)]
     halves = jax.ShapeDtypeStruct((2, 9, S, 256), F32)
     anywhere = [pl.BlockSpec(memory_space=pl.ANY)] * 2
     done = pl.pallas_call(
         functools.partial(kernel, count, 4 if count % 4 == 0 else 1),
-        out_shape=[halves, jax.ShapeDtypeStruct((count, 5, 128), F32)],
+        out_shape=[halves, shapes[1]],
         in_specs=[pl.BlockSpec(memory_space=pltpu.HBM)] * 5,
-        out_specs=tuple(anywhere),
+        out_specs=(anywhere[0], vmem(1)[0]),
         scratch_shapes=scratch,
         compiler_params=pltpu.CompilerParams(vmem_limit_bytes=32 * 2**20, collective_id=0, has_side_effects=True),
     )(*[pltpu.with_memory_space_constraint(x, pltpu.HBM) for x in (diffusivity, mixing, loss_matrix, pair_matrix, previous)])
     return tuple(pl.pallas_call(
         put_out,
         out_shape=shapes,
-        in_specs=anywhere[:1] + vmem(1),
-        out_specs=(anywhere[0], vmem(1)[0]),
-        scratch_shapes=[pltpu.SemaphoreType.DMA((2,))],
+        in_specs=anywhere,
+        out_specs=tuple(anywhere),
+        scratch_shapes=[pltpu.SemaphoreType.DMA((3,))],
         compiler_params=pltpu.CompilerParams(vmem_limit_bytes=8 * 2**20),
     )(*done))
 

time: 52.3 us -> 50.9 us (0.973)
  Pallas kernels: 51.4 us -> 50 us
    pallas_call x1, Pallas kernels: 49.8 us -> 49 us  [local(): pl.pallas_call(functools.partial(kernel, count, 4 if count % 4 == 0 else...]
    pallas_call x1, Pallas kernels: 1.63 us -> 1.04 us  [local(): pl.pallas_call(put_out, out_shape=shapes, in_specs=anywhere, out_specs=tu...]
where the time goes in v5:
time: 50.9 us; the launch traced here: 50.8 us
  Pallas kernels  50 us (98%)
  between operations  0.8 us (2%)
    pallas_call x1, Pallas kernels, local(): pl.pallas_call(functools.partial(kernel, count, 4 if count % 4 == 0 else...  49 us
    pallas_call x1, Pallas kernels, local(): pl.pallas_call(put_out, out_shape=shapes, in_specs=anywhere, out_specs=tu...  1.04 us

profile of v5, /device:TPU:1, one launch (start us, length us, event | category | flops | bytes accessed | tf_op | source)
XLA Modules:
  0.0 50.8 jit_solution(11044700973562862416)
XLA Ops:
  0.6 49.0 %shard_map.68 = (f32[2,9,64,256]{3,2,1,0:T(8,128)S(1)}, f32[9,64]{1,0:T(8,128)S(1)}) custom-call(f32[9]{0:T(128)} %link_hbm.1, f32[9]{0:T(128)} %mix_hbm.1, f32[9,64,64]{2,1,0:T(8,128)} %loss_hbm.1, f32[9,64,64]{2,1,0:T(8,128)} %pair_hbm.1, f32[9,64,512]{2,1,0:T(8,128)} %prev_hbm.1), custom_call_target="tpu_custom_call" | custom-call | tf_op jit(solution)/shard_map/pallas_call | solution.py:555
  49.6 1.0 %shard_map.69 = (f32[9,64,512]{2,1,0:T(8,128)}, f32[9,64]{1,0:T(8,128)}) custom-call(f32[2,9,64,256]{3,2,1,0:T(8,128)S(1)} %get-tuple-element.4.field_any, f32[9,64]{1,0:T(8,128)S(1)} %get-tuple-element.5.sums_any), custom_call_target="tpu_custom_call" | custom-call | tf_op jit(solution)/shard_map/pallas_call | solution.py:563

commit v6 on v5

--- a/solution.py
+++ b/solution.py
@@ -57,17 +57,20 @@
             terms[i] = twice
             centre = centres[i]
             n = unit.shape[0]
-            rest = split(residuals[i])
+            late = step >= doublings - 2
+            parts = (lambda x: (x.astype(BF16),)) if late else split
+            product = (lambda x, y: lax.dot_general(x[0], y[0], NN, preferred_element_type=F32)) if late else dot3
+            rest = parts(residuals[i])
             if step == 0:
                 inverses[i] = (inverses[i] + residuals[i] * (1.0 / centre)) * gain
                 if not last:
-                    residuals[i] = gain * dot3(rest, rest) - shift * unit
+                    residuals[i] = gain * product(rest, rest) - shift * unit
                 continue
-            known = split(inverses[i])
+            known = parts(inverses[i])
             if last:
-                inverses[i] = gain * (inverses[i] + dot3(known, rest))
+                inverses[i] = gain * (inverses[i] + product(known, rest))
                 continue
-            both = dot3(tuple(jnp.concatenate(p, axis=0) for p in zip(known, rest)), rest)
+            both = product(tuple(jnp.concatenate(p, axis=0) for p in zip(known, rest)), rest)
             inverses[i] = gain * (inverses[i] + both[:n])
             residuals[i] = gain * both[n:] - shift * unit
     exact = [unit - mm_full(block, inverse) for unit, block, inverse in zip(units, blocks, inverses)]
@@ -261,7 +264,7 @@
            link_ref, mix_ref, loss_ref, pair_ref, prev_ref, load_sem,
            full, row, g_hi, g_lo, hr_hi, hr_lo, hc_hi, hc_lo, pack, pw_hi, pw_lo, pn_hi, pn_lo, field, mixrow,
            packs, own_hi, own_lo, msg_hi, msg_lo, rlo_hi, rlo_lo, rhi_hi, rhi_lo, wp, wc, rs, rc, own,
-           state, gs_hi, gs_lo, injs, outgo, incoming, sums, outs, part, part_in, mysum, sumbuf,
+           state, gs_hi, gs_lo, injs, outgo, incoming, sums, outs, ends_ref, part, part_in, mysum, sumbuf,
            pack_send, pack_recv, give_send, give_recv, halo_send, halo_recv, msg_send, msg_recv, out_send, out_recv,
            sum_send, sum_recv):
     lev = lax.axis_index("lev")
@@ -349,7 +352,6 @@
     ]
     state[0, core, rows_at(8 * away, 264), :] = field[rows_at(248 * core, 264), :]
     finish_interior(*parts, full.at[core])
-    give_full = start(remote(full.at[core], full.at[core], give_send.at[4], give_recv.at[4], {"lev": partner}))
 
     def pair_term(it, s):
         for r in range(0, 256, 128):
@@ -400,6 +402,7 @@
     pair_term(0, away)
     forcing_term(0, away, middle)
     handed.append(hand_on(0, 2))
+    give_full = start(remote(full.at[core], full.at[core], give_send.at[4], give_recv.at[4], {"lev": partner}))
     for slot in range(2):
         pltpu.make_async_copy(field.at[0:8], state.at[0, 0, 0:8], halo_recv.at[0, slot]).wait()
     for s in range(2):
@@ -467,17 +470,20 @@
             for s in range(2):
                 land(s, 16, 240)
             continue
-        for s in range(2):
-            pieces = split(total_of[s])
-            for b in range(4):
-                rows = slice(128 * b, 128 * b + 128)
-                value = dot3((hc_hi[s, rows, :], hc_lo[s, rows, :]), pieces, NT)
-                for h in range(2):
-                    outs[s, ORDER[2 * b + h]] += value[64 * h : 64 * h + 64]
-            outs[s, 0] = total_of[s].T[0:64]
     ones = jnp.ones((8, 256), BF16)
     dot1 = lambda x: lax.dot_general(ones, x, NT, preferred_element_type=F32)
     line = lax.broadcasted_iota(jnp.int32, (8, 128), 0)
+
+    ends_ref[0], ends_ref[1] = total_of
+
+    def last_values(s):
+        pieces = split(ends_ref[s])
+        for b in range(4):
+            rows = slice(128 * b, 128 * b + 128)
+            value = dot3((hc_hi[s, rows, :], hc_lo[s, rows, :]), pieces, NT)
+            for h in range(2):
+                outs[s, ORDER[2 * b + h]] += value[64 * h : 64 * h + 64]
+        outs[s, 0] = ends_ref[s].T[0:64]
 
     def squares_of(s):
         packed = jnp.zeros((8, 128), F32)
@@ -488,9 +494,11 @@
             packed = jnp.where(line == j, dot1(high) + dot1(low), packed)
         part[s] = packed
 
+    last_values(away)
     squares_of(away)
     give = start(remote(part.at[away], part_in, out_send.at[0], out_recv.at[0], {"lev": partner}))
     back = start(remote(outs.at[away], out_any.at[core], out_send.at[1], out_recv.at[1], {"lev": partner}))
+    last_values(core)
     keep = pltpu.make_async_copy(outs.at[core], out_any.at[core], load_sem.at[0])
     keep.start()
     squares_of(core)
@@ -504,16 +512,16 @@
     for i, (dy, dz) in enumerate(steps):
         target = lax.rem(y + dy, deep) * wide_z + lax.rem(z + dz, wide_z)
         slot = lax.rem(count + lon - target - 1, count)
-        remote(mysum, sumbuf.at[slot], sum_send, sum_recv, {"lon": target}).start()
+        remote(mysum.at[0:5], sumbuf.at[slot, 0:5], sum_send, sum_recv, {"lon": target}).start()
     keep.wait()
     back.wait_recv()
     for copy in pending:
         copy.wait_send()
     if steps:
-        slots = sumbuf.at[0 : len(steps)]
+        slots = sumbuf.at[0 : len(steps), 0:5]
         pltpu.make_async_copy(slots, slots, sum_send).wait()
         pltpu.make_async_copy(slots, slots, sum_recv).wait()
-        mine = mine + jnp.sum(sumbuf[...], axis=0)
+        mine = mine[0:5] + jnp.sum(sumbuf[:, 0:5], axis=0)
     total = mine * (1.0 / (512 * count))
     for j in range(9):
         level = (ORDER + (0,))[j]
@@ -522,10 +530,13 @@
 
 def put_out(field_any, sums_any, out_ref, var_ref, sem):
     copies = [
-        pltpu.make_async_copy(field_any.at[half], out_ref.at[:, :, pl.ds(256 * half, 256)], sem.at[half])
+        pltpu.make_async_copy(
+            field_any.at[half, pl.ds(level, 3)], out_ref.at[pl.ds(level, 3), :, pl.ds(256 * half, 256)], sem.at[3 * half + level // 3]
+        )
         for half in range(2)
+        for level in (0, 3, 6)
     ]
-    copies.append(pltpu.make_async_copy(sums_any, var_ref, sem.at[2]))
+    copies.append(pltpu.make_async_copy(sums_any, var_ref, sem.at[6]))
     for copy in copies:
         copy.start()
     for copy in copies:
@@ -547,7 +558,7 @@
     scratch += full(8, 96, 128) + low(256, 256) + low(512, 256) + low(256, 256) * 2
     scratch += full(256, S) * 2 + full(S, 256) * 2 + full(256, 256)
     scratch += full(2, 2, 272, 640) + low(2, 256, 512) + full(2, 256, 128) + full(2, 2, 128, 128) + full(2, 3, 128, 128)
-    scratch += full(2, 256, 640) + full(2, 9, S, 256) + full(2, 8, 128) + full(8, 128) * 2 + full(max(count - 1, 1), 8, 128)
+    scratch += full(2, 256, 640) + full(2, 9, S, 256) + full(2, 256, 128) + full(2, 8, 128) + full(8, 128) * 2 + full(max(count - 1, 1), 8, 128)
     scratch += sems(7) + sems(5) + sems(2, 2) + sems(2, 3) + sems(2) + [pltpu.SemaphoreType.DMA] * 2
     shapes = [jax.ShapeDtypeStruct((9, S, 512), F32), jax.ShapeDtypeStruct((9, S), F32)]
     halves = jax.ShapeDtypeStruct((2, 9, S, 256), F32)
@@ -565,7 +576,7 @@
         out_shape=shapes,
         in_specs=anywhere,
         out_specs=tuple(anywhere),
-        scratch_shapes=[pltpu.SemaphoreType.DMA((3,))],
+        scratch_shapes=[pltpu.SemaphoreType.DMA((7,))],
         compiler_params=pltpu.CompilerParams(vmem_limit_bytes=8 * 2**20),
     )(*done))
 

time: 50.9 us -> 49.2 us (0.967)
  Pallas kernels: 50 us -> 48.3 us
    pallas_call x1, Pallas kernels: 49 us -> 47.2 us  [local(): pl.pallas_call(functools.partial(kernel, count, 4 if count % 4 == 0 else...]
where the time goes in v6:
time: 49.2 us; the launch traced here: 49.1 us
  Pallas kernels  48.3 us (98%)
  between operations  0.8 us (2%)
    pallas_call x1, Pallas kernels, local(): pl.pallas_call(functools.partial(kernel, count, 4 if count % 4 == 0 else...  47.2 us
    pallas_call x1, Pallas kernels, local(): pl.pallas_call(put_out, out_shape=shapes, in_specs=anywhere, out_specs=tu...  1.07 us

profile of v6, /device:TPU:1, one launch (start us, length us, event | category | flops | bytes accessed | tf_op | source)
XLA Modules:
  0.0 49.1 jit_solution(10223856284534548814)
XLA Ops:
  0.6 47.2 %shard_map.68 = (f32[2,9,64,256]{3,2,1,0:T(8,128)S(1)}, f32[9,64]{1,0:T(8,128)S(1)}) custom-call(f32[9]{0:T(128)} %link_hbm.1, f32[9]{0:T(128)} %mix_hbm.1, f32[9,64,64]{2,1,0:T(8,128)} %loss_hbm.1, f32[9,64,64]{2,1,0:T(8,128)} %pair_hbm.1, f32[9,64,512]{2,1,0:T(8,128)} %prev_hbm.1), custom_call_target="tpu_custom_call" | custom-call | tf_op jit(solution)/shard_map/pallas_call | solution.py:566
  47.8 1.1 %shard_map.69 = (f32[9,64,512]{2,1,0:T(8,128)}, f32[9,64]{1,0:T(8,128)}) custom-call(f32[2,9,64,256]{3,2,1,0:T(8,128)S(1)} %get-tuple-element.4.field_any, f32[9,64]{1,0:T(8,128)S(1)} %get-tuple-element.5.sums_any), custom_call_target="tpu_custom_call" | custom-call | tf_op jit(solution)/shard_map/pallas_call | solution.py:574

commit v7 on v6

--- a/solution.py
+++ b/solution.py
@@ -11,7 +11,6 @@
 F32 = jnp.float32
 BF16 = jnp.bfloat16
 MESH = pl.DeviceIdType.MESH
-HIGHEST = lax.Precision.HIGHEST
 
 S = 64
 ORDER = (1, 2, 4, 5, 7, 8, 3, 6)
@@ -32,10 +31,6 @@
 
 def mm(a, b, dims=NN):
     return dot3(split(a), split(b), dims)
-
-
-def mm_full(a, b, dims=NN):
-    return lax.dot_general(a, b, dims, precision=HIGHEST, preferred_element_type=F32)
 
 
 def eye(n):
@@ -73,7 +68,7 @@
             both = product(tuple(jnp.concatenate(p, axis=0) for p in zip(known, rest)), rest)
             inverses[i] = gain * (inverses[i] + both[:n])
             residuals[i] = gain * both[n:] - shift * unit
-    exact = [unit - mm_full(block, inverse) for unit, block, inverse in zip(units, blocks, inverses)]
+    exact = [unit - mm(block, inverse) for unit, block, inverse in zip(units, blocks, inverses)]
     step = lambda x, y: lax.dot_general(x.astype(BF16), y.astype(BF16), NN, preferred_element_type=F32)
     return [inverse + step(inverse, rest) for inverse, rest in zip(inverses, exact)]
 
@@ -82,7 +77,7 @@
     return jnp.concatenate([jnp.concatenate(row, axis=1) if len(row) > 1 else row[0] for row in grid], axis=0)
 
 
-def interior(link_ref, loss_ref, row_ref, pack_ref):
+def interior(link_ref, loss_ref, pack_ref):
     one = eye(S)
     zero = jnp.zeros((S, S), F32)
     links = [link_ref[i] for i in range(9)]
@@ -101,27 +96,34 @@
     ground = jnp.concatenate(
         [shunt[1] + links[0] * one, shunt[2], shunt[4], shunt[5], shunt[7], shunt[8] + links[8] * one], axis=0
     )
-    own = jnp.concatenate([shunt[3], shunt[6]], axis=0) + mm_full(spread, ground)
+    own = jnp.concatenate([shunt[3], shunt[6]], axis=0) + mm(spread, ground)
     down = links[5] * spread[0:S, 192:256]
     up = links[3] * spread[S:, 128:192]
+    lane = lax.broadcasted_iota(jnp.int32, (128, 128), 1)
+    ends = jnp.where(lane < S, spread[:, 0:128], spread[:, 256:384])
+    stack = jnp.concatenate([shunt[level] for level in ORDER], axis=0)
+    through = mm(spread, stack[0:384]) + stack[384:512]
+    direct = [mm(pairs[0][:S], stack[0:128]), mm(pairs[2][S:], stack[256:384])]
     middle, = spd_inverses([wide([[own[:S] + down, -down], [-up, own[S:] + up]])], [68.6], 3010.0, 5)
-    spread = jnp.concatenate([spread, eye(128)], axis=1)
-    lifted = mm(middle, spread)
-    lane = lax.broadcasted_iota(jnp.int32, (128, 128), 1)
-    ends = mm(jnp.where(lane < S, spread[:, 0:128], spread[:, 256:384]), lifted, TN)
+    seen = mm(ends, middle, TN)
+    loads = mm(seen, through)
+    across = (links[0] * links[8]) * mm(seen[0:S], spread)[:, 320:384]
+    pack_ref[0:64, :] = jnp.concatenate(
+        [shunt[0] + links[0] * (loads[0:S] + direct[0]), links[8] * (loads[S:] + direct[1])], axis=1
+    )
+    pack_ref[64:96, :] = jnp.concatenate([across[0:32], across[32:64]], axis=1)
+    return pairs, jnp.concatenate([spread, eye(128)], axis=1), middle, seen
+
+
+def end_rows(link_ref, row_ref, pairs, spread, middle, seen):
+    ends = mm(seen, spread)
     first = jnp.concatenate([ends[0:S, 0:128] + pairs[0][:S], ends[0:S, 128:512]], axis=1)
     last = jnp.concatenate([ends[S:, 0:256], ends[S:, 256:384] + pairs[2][S:], ends[S:, 384:512]], axis=1)
-    rows = jnp.concatenate([links[0] * first, links[8] * last], axis=0)
-    row_ref[...] = rows
-    loads = mm_full(rows, jnp.concatenate([shunt[level] for level in ORDER], axis=0))
-    across = links[8] * rows[0:S, 320:384]
-    pack_ref[0:64, :] = jnp.concatenate([shunt[0] + loads[0:S], loads[S:]], axis=1)
-    pack_ref[64:96, :] = jnp.concatenate([across[0:32], across[32:64]], axis=1)
-    return pairs, spread, lifted
-
-
-def finish_interior(pairs, spread, lifted, full):
-    full[...] = mm(spread, lifted, TN)
+    row_ref[...] = jnp.concatenate([link_ref[0] * first, link_ref[8] * last], axis=0)
+
+
+def finish_interior(full, pairs, spread, middle, seen):
+    full[...] = mm(spread, mm(middle, spread), TN)
     for i in range(3):
         at = slice(128 * i, 128 * i + 128)
         full[at, at] += pairs[i]
@@ -192,8 +194,8 @@
     lower_t = mm(across[4], lower_inverse[0:64, :])
     middle = (
         ground[4]
-        + mm_full(upper_t, jnp.concatenate(ground[0:4], axis=0))
-        + mm_full(lower_t, jnp.concatenate([ground[5], ground[6], ground[7] + across[7]], axis=0))
+        + mm(upper_t, jnp.concatenate(ground[0:4], axis=0))
+        + mm(lower_t, jnp.concatenate([ground[5], ground[6], ground[7] + across[7]], axis=0))
     )
     middle_inverse, = spd_inverses([middle], [28.7], 2400.0, 5)
     spread = jnp.concatenate([upper_t, lower_t, one], axis=1)
@@ -264,7 +266,7 @@
            link_ref, mix_ref, loss_ref, pair_ref, prev_ref, load_sem,
            full, row, g_hi, g_lo, hr_hi, hr_lo, hc_hi, hc_lo, pack, pw_hi, pw_lo, pn_hi, pn_lo, field, mixrow,
            packs, own_hi, own_lo, msg_hi, msg_lo, rlo_hi, rlo_lo, rhi_hi, rhi_lo, wp, wc, rs, rc, own,
-           state, gs_hi, gs_lo, injs, outgo, incoming, sums, outs, ends_ref, part, part_in, mysum, sumbuf,
+           state, gs_hi, gs_lo, injs, outgo, incoming, out_most, in_most, out_edge, in_edge, sums, outs, ends_ref, part, part_in, mysum, sumbuf,
            pack_send, pack_recv, give_send, give_recv, halo_send, halo_recv, msg_send, msg_recv, out_send, out_recv,
            sum_send, sum_recv):
     lev = lax.axis_index("lev")
@@ -316,7 +318,7 @@
 
     loads[0].wait()
     loads[1].wait()
-    parts = interior(link_ref, loss_ref, row.at[core], pack)
+    parts = interior(link_ref, loss_ref, pack)
     loads[3].wait()
     loads[4].wait()
     mix_row_of(mix_ref, mixrow.at[core])
@@ -326,6 +328,7 @@
         start(remote(pack, packs.at[lev], pack_send.at[i], pack_recv.at[i], {"lev": target}))
         for i, target in enumerate([2 * lax.rem(chip + d, 4) + core for d in (2, 1, 3)] + [partner])
     ]
+    end_rows(link_ref, row.at[core], *parts)
     loads[2].wait()
     field_of(prev_ref, field)
 
@@ -351,29 +354,33 @@
                      {"lev": base, "lon": east})),
     ]
     state[0, core, rows_at(8 * away, 264), :] = field[rows_at(248 * core, 264), :]
-    finish_interior(*parts, full.at[core])
+    finish_interior(full.at[core], *parts)
 
     def pair_term(it, s):
-        for r in range(0, 256, 128):
-            here = state[it, s, 8 + r : 136 + r, :]
-            squares = split(here * here)
-            for half in range(2):
-                piece = tuple(x[:, 256 * half : 256 * half + 256] for x in squares)
-                sums[s, r : r + 128, 256 * half : 256 * half + 256] = dot3(piece, (pw_hi[s, half], pw_lo[s, half]), NT)
-            piece = tuple(x[:, 512:576] for x in squares)
-            sums[s, r : r + 128, 512:576] = dot3(piece, (pn_hi[s], pn_lo[s]), NT)
-
-    def forcing_term(it, s, chunks=((0, 128), (128, 128))):
+        here = state[it, s, 8:264, :]
+        squares = split(here * here)
+        for half in range(2):
+            piece = tuple(x[:, 256 * half : 256 * half + 256] for x in squares)
+            sums[s, :, 256 * half : 256 * half + 256] = dot3(piece, (pw_hi[s, half], pw_lo[s, half]), NT)
+        piece = tuple(x[:, 512:576] for x in squares)
+        sums[s, :, 512:576] = dot3(piece, (pn_hi[s], pn_lo[s]), NT)
+
+    def forcing_term(it, s, chunks):
+        forcing = []
         for r, n in chunks:
             here = state[it, s, 8 + r : 8 + r + n, 0:576]
             around = state[it, s, 7 + r : 7 + r + n, 0:576] + state[it, s, 9 + r : 9 + r + n, 0:576]
-            forcing = state[0, s, 8 + r : 8 + r + n, 0:576] - sums[s, r : r + n, 0:576]
-            forcing += mixrow[s, 0:1, 0:576] * (around - 2.0 * here)
-            pieces = split(forcing[:, 0:512])
-            gs_hi[s, r : r + n, :], gs_lo[s, r : r + n, :] = pieces
-            node = forcing[:, 512:576]
-            push = dot3(pieces, (hr_hi[s], hr_lo[s]), NT)
-            injs[s, r : r + n, :] = push + jnp.concatenate([node, jnp.zeros_like(node)], axis=1)
+            value = state[0, s, 8 + r : 8 + r + n, 0:576] - sums[s, r : r + n, 0:576]
+            forcing.append(value + mixrow[s, 0:1, 0:576] * (around - 2.0 * here))
+        forcing = jnp.concatenate(forcing, axis=0) if len(forcing) > 1 else forcing[0]
+        pieces = split(forcing[:, 0:512])
+        node = forcing[:, 512:576]
+        push = dot3(pieces, (hr_hi[s], hr_lo[s]), NT) + jnp.concatenate([node, jnp.zeros_like(node)], axis=1)
+        at = 0
+        for r, n in chunks:
+            gs_hi[s, r : r + n, :], gs_lo[s, r : r + n, :] = (x[at : at + n] for x in pieces)
+            injs[s, r : r + n, :] = push[at : at + n]
+            at += n
 
     def weights(s):
         pair_weights(pair_ref.at[s], pw_hi.at[s], pw_lo.at[s], pn_hi.at[s], pn_lo.at[s])
@@ -387,11 +394,9 @@
                 for h in range(2):
                     outs[s, ORDER[2 * b + h]] = value[64 * h : 64 * h + 64]
         else:
-            for r in range(0, 256, 128):
-                pieces = (gs_hi[s, r : r + 128, :], gs_lo[s, r : r + 128, :])
-                state[it + 1, s, 8 + r : 136 + r, 0:512] = dot3(pieces, (g_hi[s], g_lo[s]))
-
-    middle, edges = ((16, 112), (128, 112)), ((0, 16), (240, 16))
+            state[it + 1, s, 8:264, 0:512] = dot3((gs_hi[s], gs_lo[s]), (g_hi[s], g_lo[s]))
+
+    middle, edges = ((16, 224),), ((0, 16), (240, 16))
     weights(core)
     pair_term(0, core)
     forcing_term(0, core, middle)
@@ -417,19 +422,29 @@
                 pair_term(it, s)
             for s in range(2):
                 forcing_term(it, s, middle)
+        slot = 1 + lax.rem(chip, 2)
+
+        def send(chunks, out, into, sems):
+            lines = [
+                jnp.concatenate([injs[s, q + r : q + r + n] for q in (0, 128) for s in range(2)], axis=1) for r, n in chunks
+            ]
+            message = dot3(split(jnp.concatenate(lines, axis=0) if len(lines) > 1 else lines[0]), (msg_hi[...], msg_lo[...]))
+            out[0] = message[:, 0:128]
+            out[1] = message[:, 128:256]
+            to = [(1, slot, {"lev": across[0]}), (1, slot, {"lev": across[1]}), (0, 0, {"lev": sibling})]
+            for i, (which, where, target) in enumerate(to):
+                start(remote(out.at[which], into.at[where], msg_send.at[sems, i], msg_recv.at[sems, where], target))
+
+        if it == 0:
+            send([(0, 128)], outgo, incoming, 0)
+        else:
+            send([(16, 96)], out_most, in_most, 1)
             for halo in halos:
                 halo.wait_recv()
             for s in range(2):
                 forcing_term(it, s, edges)
+            send([(0, 16), (112, 16)], out_edge, in_edge, 2)
         inj = jnp.concatenate([injs[0], injs[1]], axis=1)
-        packed = split(jnp.concatenate([inj[0:128], inj[128:256]], axis=1))
-        message = dot3(packed, (msg_hi[...], msg_lo[...]))
-        outgo[it, 0] = message[:, 0:128]
-        outgo[it, 1] = message[:, 128:256]
-        slot = 1 + lax.rem(chip, 2)
-        start(remote(outgo.at[it, 1], incoming.at[it, slot], msg_send.at[it, 1], msg_recv.at[it, slot], {"lev": across[0]}))
-        start(remote(outgo.at[it, 1], incoming.at[it, slot], msg_send.at[it, 2], msg_recv.at[it, slot], {"lev": across[1]}))
-        start(remote(outgo.at[it, 0], incoming.at[it, 0], msg_send.at[it, 0], msg_recv.at[it, 0], {"lev": sibling}))
         mine = dot3(split(inj), (own_hi[...], own_lo[...]))
         if it == 0:
             give_full.wait_recv()
@@ -438,25 +453,33 @@
                 hc_hi[s], hc_lo[s] = split(row[s].T)
         for s in range(2):
             product(it, s)
-        for slot in range(3):
-            pltpu.make_async_copy(outgo.at[it, 0], incoming.at[it, slot], msg_recv.at[it, slot]).wait()
-        heard = split(jnp.concatenate([incoming[it, 0], incoming[it, 1] + incoming[it, 2]], axis=1))
+        for i, into in [(0, incoming)] if it == 0 else [(1, in_most), (2, in_edge)]:
+            for where in range(3):
+                pltpu.make_async_copy(into.at[where], into.at[where], msg_recv.at[i, where]).wait()
+        join = lambda x: jnp.concatenate([x[0], x[1] + x[2]], axis=1)
+        if it == 0:
+            heard = join(incoming)
+        else:
+            heard = jnp.concatenate([join(in_edge[:, 0:16]), join(in_most), join(in_edge[:, 16:32])], axis=0)
+        heard = split(heard)
         total = mine + jnp.concatenate(
             [dot3(heard, (rlo_hi[...], rlo_lo[...])), dot3(heard, (rhi_hi[...], rhi_lo[...]))], axis=0
         )
         total_of = [total[:, 128 * s : 128 * s + 128] for s in range(2)]
         if not final:
-            def land(s, low, high):
-                ends = total_of[s][low:high]
-                rows = slice(8 + low, 8 + high)
-                state[it + 1, s, rows, 0:512] += dot3(split(ends), (hr_hi[s], hr_lo[s]))
-                state[it + 1, s, rows, 512:640] = jnp.where(
-                    lax.broadcasted_iota(jnp.int32, (high - low, 128), 1) < S, ends, 0.0
-                )
+            def land(s, chunks):
+                ends = [total_of[s][r : r + n] for r, n in chunks]
+                ends = jnp.concatenate(ends, axis=0) if len(ends) > 1 else ends[0]
+                add = dot3(split(ends), (hr_hi[s], hr_lo[s]))
+                node = jnp.where(lax.broadcasted_iota(jnp.int32, ends.shape, 1) < S, ends, 0.0)
+                at = 0
+                for r, n in chunks:
+                    state[it + 1, s, 8 + r : 8 + r + n, 0:512] += add[at : at + n]
+                    state[it + 1, s, 8 + r : 8 + r + n, 512:640] = node[at : at + n]
+                    at += n
 
             for s in range(2):
-                land(s, 0, 16)
-                land(s, 240, 256)
+                land(s, edges)
             inner_from, inner_to = 8 + 248 * away, 264 * core
             outer_from, outer_to = 8 + 248 * core, 264 * away
             halos = [
@@ -468,7 +491,7 @@
                 ])
             ]
             for s in range(2):
-                land(s, 16, 240)
+                land(s, middle)
             continue
     ones = jnp.ones((8, 256), BF16)
     dot1 = lambda x: lax.dot_general(ones, x, NT, preferred_element_type=F32)
@@ -557,9 +580,10 @@
     scratch += low(2, 2, 256, 256) + low(2, S, S) + full(512, 640) + full(2, 8, 640)
     scratch += full(8, 96, 128) + low(256, 256) + low(512, 256) + low(256, 256) * 2
     scratch += full(256, S) * 2 + full(S, 256) * 2 + full(256, 256)
-    scratch += full(2, 2, 272, 640) + low(2, 256, 512) + full(2, 256, 128) + full(2, 2, 128, 128) + full(2, 3, 128, 128)
+    scratch += full(2, 2, 272, 640) + low(2, 256, 512) + full(2, 256, 128) + full(2, 128, 128) + full(3, 128, 128)
+    scratch += full(2, 96, 128) + full(3, 96, 128) + full(2, 32, 128) + full(3, 32, 128)
     scratch += full(2, 256, 640) + full(2, 9, S, 256) + full(2, 256, 128) + full(2, 8, 128) + full(8, 128) * 2 + full(max(count - 1, 1), 8, 128)
-    scratch += sems(7) + sems(5) + sems(2, 2) + sems(2, 3) + sems(2) + [pltpu.SemaphoreType.DMA] * 2
+    scratch += sems(7) + sems(5) + sems(2, 2) + sems(3, 3) + sems(2) + [pltpu.SemaphoreType.DMA] * 2
     shapes = [jax.ShapeDtypeStruct((9, S, 512), F32), jax.ShapeDtypeStruct((9, S), F32)]
     halves = jax.ShapeDtypeStruct((2, 9, S, 256), F32)
     anywhere = [pl.BlockSpec(memory_space=pl.ANY)] * 2

time: 49.2 us -> 46.4 us (0.943)
  Pallas kernels: 48.3 us -> 45.5 us
    pallas_call x1, Pallas kernels: 47.2 us -> 44.4 us  [local(): pl.pallas_call(functools.partial(kernel, count, 4 if count % 4 == 0 else...]
where the time goes in v7:
time: 46.4 us; the launch traced here: 46.3 us
  Pallas kernels  45.5 us (98%)
  between operations  0.8 us (2%)
    pallas_call x1, Pallas kernels, local(): pl.pallas_call(functools.partial(kernel, count, 4 if count % 4 == 0 else...  44.4 us
    pallas_call x1, Pallas kernels, local(): pl.pallas_call(put_out, out_shape=shapes, in_specs=anywhere, out_specs=tu...  1.07 us

profile of v7, /device:TPU:1, one launch (start us, length us, event | category | flops | bytes accessed | tf_op | source)
XLA Modules:
  0.0 46.3 jit_solution(12414642116316086069)
XLA Ops:
  0.6 44.4 %shard_map.68 = (f32[2,9,64,256]{3,2,1,0:T(8,128)S(1)}, f32[9,64]{1,0:T(8,128)S(1)}) custom-call(f32[9]{0:T(128)} %link_hbm.1, f32[9]{0:T(128)} %mix_hbm.1, f32[9,64,64]{2,1,0:T(8,128)} %loss_hbm.1, f32[9,64,64]{2,1,0:T(8,128)} %pair_hbm.1, f32[9,64,512]{2,1,0:T(8,128)} %prev_hbm.1), custom_call_target="tpu_custom_call" | custom-call | tf_op jit(solution)/shard_map/pallas_call | solution.py:590
  45.0 1.1 %shard_map.69 = (f32[9,64,512]{2,1,0:T(8,128)}, f32[9,64]{1,0:T(8,128)}) custom-call(f32[2,9,64,256]{3,2,1,0:T(8,128)S(1)} %get-tuple-element.4.field_any, f32[9,64]{1,0:T(8,128)S(1)} %get-tuple-element.5.sums_any), custom_call_target="tpu_custom_call" | custom-call | tf_op jit(solution)/shard_map/pallas_call | solution.py:598

commit v8 on v7

--- a/solution.py
+++ b/solution.py
@@ -52,7 +52,7 @@
             terms[i] = twice
             centre = centres[i]
             n = unit.shape[0]
-            late = step >= doublings - 2
+            late = step >= doublings - 3
             parts = (lambda x: (x.astype(BF16),)) if late else split
             product = (lambda x, y: lax.dot_general(x[0], y[0], NN, preferred_element_type=F32)) if late else dot3
             rest = parts(residuals[i])
@@ -266,7 +266,7 @@
            link_ref, mix_ref, loss_ref, pair_ref, prev_ref, load_sem,
            full, row, g_hi, g_lo, hr_hi, hr_lo, hc_hi, hc_lo, pack, pw_hi, pw_lo, pn_hi, pn_lo, field, mixrow,
            packs, own_hi, own_lo, msg_hi, msg_lo, rlo_hi, rlo_lo, rhi_hi, rhi_lo, wp, wc, rs, rc, own,
-           state, gs_hi, gs_lo, injs, outgo, incoming, out_most, in_most, out_edge, in_edge, sums, outs, ends_ref, part, part_in, mysum, sumbuf,
+           state, gs_hi, gs_lo, injs, out_first, in_first, out_then, in_then, out_most, in_most, out_edge, in_edge, sums, outs, ends_ref, part, part_in, mysum, sumbuf,
            pack_send, pack_recv, give_send, give_recv, halo_send, halo_recv, msg_send, msg_recv, out_send, out_recv,
            sum_send, sum_recv):
     lev = lax.axis_index("lev")
@@ -356,14 +356,21 @@
     state[0, core, rows_at(8 * away, 264), :] = field[rows_at(248 * core, 264), :]
     finish_interior(full.at[core], *parts)
 
-    def pair_term(it, s):
-        here = state[it, s, 8:264, :]
+    def pair_term(it, s, chunks=((0, 256),)):
+        here = [state[it, s, 8 + r : 8 + r + n, :] for r, n in chunks]
+        here = jnp.concatenate(here, axis=0) if len(here) > 1 else here[0]
         squares = split(here * here)
+        out = []
         for half in range(2):
             piece = tuple(x[:, 256 * half : 256 * half + 256] for x in squares)
-            sums[s, :, 256 * half : 256 * half + 256] = dot3(piece, (pw_hi[s, half], pw_lo[s, half]), NT)
+            out.append((256 * half, 256, dot3(piece, (pw_hi[s, half], pw_lo[s, half]), NT)))
         piece = tuple(x[:, 512:576] for x in squares)
-        sums[s, :, 512:576] = dot3(piece, (pn_hi[s], pn_lo[s]), NT)
+        out.append((512, 64, dot3(piece, (pn_hi[s], pn_lo[s]), NT)))
+        at = 0
+        for r, n in chunks:
+            for lane, width, value in out:
+                sums[s, r : r + n, lane : lane + width] = value[at : at + n]
+            at += n
 
     def forcing_term(it, s, chunks):
         forcing = []
@@ -405,8 +412,8 @@
     weights(away)
     handed = [hand_on(1, 1), hand_on(2, 3)]
     pair_term(0, away)
+    handed.append(hand_on(0, 2))
     forcing_term(0, away, middle)
-    handed.append(hand_on(0, 2))
     give_full = start(remote(full.at[core], full.at[core], give_send.at[4], give_recv.at[4], {"lev": partner}))
     for slot in range(2):
         pltpu.make_async_copy(field.at[0:8], state.at[0, 0, 0:8], halo_recv.at[0, slot]).wait()
@@ -419,31 +426,33 @@
         final = it == ITERS - 1
         if it:
             for s in range(2):
-                pair_term(it, s)
-            for s in range(2):
                 forcing_term(it, s, middle)
         slot = 1 + lax.rem(chip, 2)
 
-        def send(chunks, out, into, sems):
+        def send(chunks, parts):
             lines = [
                 jnp.concatenate([injs[s, q + r : q + r + n] for q in (0, 128) for s in range(2)], axis=1) for r, n in chunks
             ]
             message = dot3(split(jnp.concatenate(lines, axis=0) if len(lines) > 1 else lines[0]), (msg_hi[...], msg_lo[...]))
-            out[0] = message[:, 0:128]
-            out[1] = message[:, 128:256]
-            to = [(1, slot, {"lev": across[0]}), (1, slot, {"lev": across[1]}), (0, 0, {"lev": sibling})]
-            for i, (which, where, target) in enumerate(to):
-                start(remote(out.at[which], into.at[where], msg_send.at[sems, i], msg_recv.at[sems, where], target))
+            at = 0
+            for out, into, sems in parts:
+                size = out.shape[1]
+                out[0] = message[at : at + size, 0:128]
+                out[1] = message[at : at + size, 128:256]
+                at += size
+                to = [(1, slot, {"lev": across[0]}), (1, slot, {"lev": across[1]}), (0, 0, {"lev": sibling})]
+                for i, (which, where, target) in enumerate(to):
+                    start(remote(out.at[which], into.at[where], msg_send.at[sems, i], msg_recv.at[sems, where], target))
 
         if it == 0:
-            send([(0, 128)], outgo, incoming, 0)
+            send([(0, 32), (96, 32), (32, 64)], [(out_first, in_first, 0), (out_then, in_then, 3)])
         else:
-            send([(16, 96)], out_most, in_most, 1)
+            send([(16, 96)], [(out_most, in_most, 1)])
             for halo in halos:
                 halo.wait_recv()
             for s in range(2):
                 forcing_term(it, s, edges)
-            send([(0, 16), (112, 16)], out_edge, in_edge, 2)
+            send([(0, 16), (112, 16)], [(out_edge, in_edge, 2)])
         inj = jnp.concatenate([injs[0], injs[1]], axis=1)
         mine = dot3(split(inj), (own_hi[...], own_lo[...]))
         if it == 0:
@@ -453,33 +462,35 @@
                 hc_hi[s], hc_lo[s] = split(row[s].T)
         for s in range(2):
             product(it, s)
-        for i, into in [(0, incoming)] if it == 0 else [(1, in_most), (2, in_edge)]:
+        join = lambda x: jnp.concatenate([x[0], x[1] + x[2]], axis=1)
+
+        def arrived(into, sems):
             for where in range(3):
-                pltpu.make_async_copy(into.at[where], into.at[where], msg_recv.at[i, where]).wait()
-        join = lambda x: jnp.concatenate([x[0], x[1] + x[2]], axis=1)
-        if it == 0:
-            heard = join(incoming)
-        else:
-            heard = jnp.concatenate([join(in_edge[:, 0:16]), join(in_most), join(in_edge[:, 16:32])], axis=0)
-        heard = split(heard)
-        total = mine + jnp.concatenate(
-            [dot3(heard, (rlo_hi[...], rlo_lo[...])), dot3(heard, (rhi_hi[...], rhi_lo[...]))], axis=0
-        )
-        total_of = [total[:, 128 * s : 128 * s + 128] for s in range(2)]
+                pltpu.make_async_copy(into.at[where], into.at[where], msg_recv.at[sems, where]).wait()
+
+        def reached(heard, chunks):
+            here = [mine[r : r + n] for r, n in chunks]
+            heard = split(heard)
+            return (jnp.concatenate(here, axis=0) if len(here) > 1 else here[0]) + jnp.concatenate(
+                [dot3(heard, (rlo_hi[...], rlo_lo[...])), dot3(heard, (rhi_hi[...], rhi_lo[...]))], axis=0
+            )
+
+        def land(s, ends, chunks):
+            ends = ends[:, 128 * s : 128 * s + 128]
+            add = dot3(split(ends), (hr_hi[s], hr_lo[s]))
+            node = jnp.where(lax.broadcasted_iota(jnp.int32, ends.shape, 1) < S, ends, 0.0)
+            at = 0
+            for r, n in chunks:
+                state[it + 1, s, 8 + r : 8 + r + n, 0:512] += add[at : at + n]
+                state[it + 1, s, 8 + r : 8 + r + n, 512:640] = node[at : at + n]
+                at += n
+
         if not final:
-            def land(s, chunks):
-                ends = [total_of[s][r : r + n] for r, n in chunks]
-                ends = jnp.concatenate(ends, axis=0) if len(ends) > 1 else ends[0]
-                add = dot3(split(ends), (hr_hi[s], hr_lo[s]))
-                node = jnp.where(lax.broadcasted_iota(jnp.int32, ends.shape, 1) < S, ends, 0.0)
-                at = 0
-                for r, n in chunks:
-                    state[it + 1, s, 8 + r : 8 + r + n, 0:512] += add[at : at + n]
-                    state[it + 1, s, 8 + r : 8 + r + n, 512:640] = node[at : at + n]
-                    at += n
-
+            arrived(in_first, 0)
+            columns = ((0, 32), (96, 32), (128, 32), (224, 32))
+            ends = reached(join(in_first), columns)
             for s in range(2):
-                land(s, edges)
+                land(s, ends, columns)
             inner_from, inner_to = 8 + 248 * away, 264 * core
             outer_from, outer_to = 8 + 248 * core, 264 * away
             halos = [
@@ -491,9 +502,21 @@
                 ])
             ]
             for s in range(2):
-                land(s, middle)
+                pair_term(it + 1, s, columns)
+            arrived(in_then, 3)
+            columns = ((32, 64), (160, 64))
+            ends = reached(join(in_then), columns)
+            for s in range(2):
+                land(s, ends, columns)
+            for s in range(2):
+                pair_term(it + 1, s, columns)
             continue
-    ones = jnp.ones((8, 256), BF16)
+        arrived(in_most, 1)
+        arrived(in_edge, 2)
+        heard = jnp.concatenate([join(in_edge[:, 0:16]), join(in_most), join(in_edge[:, 16:32])], axis=0)
+        total = reached(heard, ((0, 256),))
+        total_of = [total[:, 128 * s : 128 * s + 128] for s in range(2)]
+    ones = jnp.ones((8, 128), BF16)
     dot1 = lambda x: lax.dot_general(ones, x, NT, preferred_element_type=F32)
     line = lax.broadcasted_iota(jnp.int32, (8, 128), 0)
 
@@ -513,7 +536,8 @@
         for j in range(5):
             values = [outs[s, level] for level in ((ORDER + (0,))[2 * j : 2 * j + 2])]
             values = jnp.concatenate(values if j < 4 else values + [jnp.zeros_like(values[0])], axis=0)
-            high, low = split(values * values)
+            values = values * values
+            high, low = split(values[:, 0:128] + values[:, 128:256])
             packed = jnp.where(line == j, dot1(high) + dot1(low), packed)
         part[s] = packed
 
@@ -580,10 +604,10 @@
     scratch += low(2, 2, 256, 256) + low(2, S, S) + full(512, 640) + full(2, 8, 640)
     scratch += full(8, 96, 128) + low(256, 256) + low(512, 256) + low(256, 256) * 2
     scratch += full(256, S) * 2 + full(S, 256) * 2 + full(256, 256)
-    scratch += full(2, 2, 272, 640) + low(2, 256, 512) + full(2, 256, 128) + full(2, 128, 128) + full(3, 128, 128)
+    scratch += full(2, 2, 272, 640) + low(2, 256, 512) + full(2, 256, 128) + full(2, 64, 128) + full(3, 64, 128) + full(2, 64, 128) + full(3, 64, 128)
     scratch += full(2, 96, 128) + full(3, 96, 128) + full(2, 32, 128) + full(3, 32, 128)
     scratch += full(2, 256, 640) + full(2, 9, S, 256) + full(2, 256, 128) + full(2, 8, 128) + full(8, 128) * 2 + full(max(count - 1, 1), 8, 128)
-    scratch += sems(7) + sems(5) + sems(2, 2) + sems(3, 3) + sems(2) + [pltpu.SemaphoreType.DMA] * 2
+    scratch += sems(7) + sems(5) + sems(2, 2) + sems(4, 3) + sems(2) + [pltpu.SemaphoreType.DMA] * 2
     shapes = [jax.ShapeDtypeStruct((9, S, 512), F32), jax.ShapeDtypeStruct((9, S), F32)]
     halves = jax.ShapeDtypeStruct((2, 9, S, 256), F32)
     anywhere = [pl.BlockSpec(memory_space=pl.ANY)] * 2

time: 46.4 us -> 45.5 us (0.981)
  Pallas kernels: 45.5 us -> 44.6 us
    pallas_call x1, Pallas kernels: 44.4 us -> 43.6 us  [local(): pl.pallas_call(functools.partial(kernel, count, 4 if count % 4 == 0 else...]
where the time goes in v8:
time: 45.5 us; the launch traced here: 45.4 us
  Pallas kernels  44.6 us (98%)
  between operations  0.8 us (2%)
    pallas_call x1, Pallas kernels, local(): pl.pallas_call(functools.partial(kernel, count, 4 if count % 4 == 0 else...  43.6 us
    pallas_call x1, Pallas kernels, local(): pl.pallas_call(put_out, out_shape=shapes, in_specs=anywhere, out_specs=tu...  1.07 us

profile of v8, /device:TPU:1, one launch (start us, length us, event | category | flops | bytes accessed | tf_op | source)
XLA Modules:
  0.0 45.4 jit_solution(9463940554842591015)
XLA Ops:
  0.6 43.6 %shard_map.68 = (f32[2,9,64,256]{3,2,1,0:T(8,128)S(1)}, f32[9,64]{1,0:T(8,128)S(1)}) custom-call(f32[9]{0:T(128)} %link_hbm.1, f32[9]{0:T(128)} %mix_hbm.1, f32[9,64,64]{2,1,0:T(8,128)} %loss_hbm.1, f32[9,64,64]{2,1,0:T(8,128)} %pair_hbm.1, f32[9,64,512]{2,1,0:T(8,128)} %prev_hbm.1), custom_call_target="tpu_custom_call" | custom-call | tf_op jit(solution)/shard_map/pallas_call | solution.py:614
  44.2 1.1 %shard_map.69 = (f32[9,64,512]{2,1,0:T(8,128)}, f32[9,64]{1,0:T(8,128)}) custom-call(f32[2,9,64,256]{3,2,1,0:T(8,128)S(1)} %get-tuple-element.4.field_any, f32[9,64]{1,0:T(8,128)S(1)} %get-tuple-element.5.sums_any), custom_call_target="tpu_custom_call" | custom-call | tf_op jit(solution)/shard_map/pallas_call | solution.py:622

commit v9 on v8

--- a/solution.py
+++ b/solution.py
@@ -328,25 +328,23 @@
         start(remote(pack, packs.at[lev], pack_send.at[i], pack_recv.at[i], {"lev": target}))
         for i, target in enumerate([2 * lax.rem(chip + d, 4) + core for d in (2, 1, 3)] + [partner])
     ]
+    away = 1 - core
+
+    def give(i, src, dst):
+        return start(remote(src, dst, give_send.at[i], give_recv.at[i], {"lev": partner}))
+
+    gives = [give(i, x.at[core], x.at[core]) for i, x in ((1, pair_ref), (2, mixrow))]
     end_rows(link_ref, row.at[core], *parts)
+    gives.append(give(3, row.at[core], row.at[core]))
     loads[2].wait()
     field_of(prev_ref, field)
+    gives.append(give(0, field.at[rows_at(248 * away, 264)], state.at[0, core, rows_at(8 * core, 264)]))
 
     def hand_on(i, d):
         spread[i].wait_recv()
         source = 2 * lax.rem(chip + 4 - d, 4) + core
         return start(remote(packs.at[source], packs.at[source], pack_send.at[4 + i], pack_recv.at[4 + i], {"lev": partner}))
 
-    away = 1 - core
-    gives = [
-        start(remote(src, dst, give_send.at[i], give_recv.at[i], {"lev": partner}))
-        for i, (src, dst) in enumerate([
-            (field.at[rows_at(248 * away, 264)], state.at[0, core, rows_at(8 * core, 264)]),
-            (pair_ref.at[core], pair_ref.at[core]),
-            (mixrow.at[core], mixrow.at[core]),
-            (row.at[core], row.at[core]),
-        ])
-    ]
     outer = [
         start(remote(field.at[0:8], state.at[0, core, 264:272], halo_send.at[0, 0], halo_recv.at[0, core],
                      {"lev": base + 1, "lon": west})),
@@ -407,18 +405,16 @@
     weights(core)
     pair_term(0, core)
     forcing_term(0, core, middle)
-    for give in gives:
-        give.wait_recv()
+    for gift in gives:
+        gift.wait_recv()
     weights(away)
-    handed = [hand_on(1, 1), hand_on(2, 3)]
     pair_term(0, away)
-    handed.append(hand_on(0, 2))
-    forcing_term(0, away, middle)
-    give_full = start(remote(full.at[core], full.at[core], give_send.at[4], give_recv.at[4], {"lev": partner}))
+    handed = [hand_on(1, 1), hand_on(2, 3), hand_on(0, 2)]
     for slot in range(2):
         pltpu.make_async_copy(field.at[0:8], state.at[0, 0, 0:8], halo_recv.at[0, slot]).wait()
-    for s in range(2):
-        forcing_term(0, s, edges)
+    forcing_term(0, core, edges)
+    forcing_term(0, away, ((0, 256),))
+    give_full = start(remote(full.at[core], full.at[core], give_send.at[4], give_recv.at[4], {"lev": partner}))
     for copy in [spread[3]] + handed:
         copy.wait_recv()
     interface(packs, own_hi, own_lo, msg_hi, msg_lo, rlo_hi, rlo_lo, rhi_hi, rhi_lo, wp, wc, rs, rc, own)

time: 45.5 us -> 45.2 us (level)
  no operation moved by 1% of the time
where the time goes in v9:
time: 45.2 us; the launch traced here: 45.1 us
  Pallas kernels  44.3 us (98%)
  between operations  0.8 us (2%)
    pallas_call x1, Pallas kernels, local(): pl.pallas_call(functools.partial(kernel, count, 4 if count % 4 == 0 else...  43.3 us
    pallas_call x1, Pallas kernels, local(): pl.pallas_call(put_out, out_shape=shapes, in_specs=anywhere, out_specs=tu...  1.07 us

profile of v9, /device:TPU:1, one launch (start us, length us, event | category | flops | bytes accessed | tf_op | source)
XLA Modules:
  0.0 45.1 jit_solution(7990556133961775127)
XLA Ops:
  0.6 43.3 %shard_map.68 = (f32[2,9,64,256]{3,2,1,0:T(8,128)S(1)}, f32[9,64]{1,0:T(8,128)S(1)}) custom-call(f32[9]{0:T(128)} %link_hbm.1, f32[9]{0:T(128)} %mix_hbm.1, f32[9,64,64]{2,1,0:T(8,128)} %loss_hbm.1, f32[9,64,64]{2,1,0:T(8,128)} %pair_hbm.1, f32[9,64,512]{2,1,0:T(8,128)} %prev_hbm.1), custom_call_target="tpu_custom_call" | custom-call | tf_op jit(solution)/shard_map/pallas_call | solution.py:610
  43.9 1.1 %shard_map.69 = (f32[9,64,512]{2,1,0:T(8,128)}, f32[9,64]{1,0:T(8,128)}) custom-call(f32[2,9,64,256]{3,2,1,0:T(8,128)S(1)} %get-tuple-element.4.field_any, f32[9,64]{1,0:T(8,128)S(1)} %get-tuple-element.5.sums_any), custom_call_target="tpu_custom_call" | custom-call | tf_op jit(solution)/shard_map/pallas_call | solution.py:618

commit v10 on v9

--- a/solution.py
+++ b/solution.py
@@ -540,7 +540,6 @@
     last_values(away)
     squares_of(away)
     give = start(remote(part.at[away], part_in, out_send.at[0], out_recv.at[0], {"lev": partner}))
-    back = start(remote(outs.at[away], out_any.at[core], out_send.at[1], out_recv.at[1], {"lev": partner}))
     last_values(core)
     keep = pltpu.make_async_copy(outs.at[core], out_any.at[core], load_sem.at[0])
     keep.start()
@@ -556,6 +555,7 @@
         target = lax.rem(y + dy, deep) * wide_z + lax.rem(z + dz, wide_z)
         slot = lax.rem(count + lon - target - 1, count)
         remote(mysum.at[0:5], sumbuf.at[slot, 0:5], sum_send, sum_recv, {"lon": target}).start()
+    back = start(remote(outs.at[away], out_any.at[core], out_send.at[1], out_recv.at[1], {"lev": partner}))
     keep.wait()
     back.wait_recv()
     for copy in pending:

time: 45.2 us -> 45.2 us (level)
  no operation moved by 1% of the time
where the time goes in v10:
time: 45.2 us; the launch traced here: 45.1 us
  Pallas kernels  44.3 us (98%)
  between operations  0.8 us (2%)
    pallas_call x1, Pallas kernels, local(): pl.pallas_call(functools.partial(kernel, count, 4 if count % 4 == 0 else...  43.3 us
    pallas_call x1, Pallas kernels, local(): pl.pallas_call(put_out, out_shape=shapes, in_specs=anywhere, out_specs=tu...  1.07 us

profile of v10, /device:TPU:1, one launch (start us, length us, event | category | flops | bytes accessed | tf_op | source)
XLA Modules:
  0.0 45.1 jit_solution(1052544168484244392)
XLA Ops:
  0.6 43.3 %shard_map.68 = (f32[2,9,64,256]{3,2,1,0:T(8,128)S(1)}, f32[9,64]{1,0:T(8,128)S(1)}) custom-call(f32[9]{0:T(128)} %link_hbm.1, f32[9]{0:T(128)} %mix_hbm.1, f32[9,64,64]{2,1,0:T(8,128)} %loss_hbm.1, f32[9,64,64]{2,1,0:T(8,128)} %pair_hbm.1, f32[9,64,512]{2,1,0:T(8,128)} %prev_hbm.1), custom_call_target="tpu_custom_call" | custom-call | tf_op jit(solution)/shard_map/pallas_call | solution.py:610
  43.9 1.1 %shard_map.69 = (f32[9,64,512]{2,1,0:T(8,128)}, f32[9,64]{1,0:T(8,128)}) custom-call(f32[2,9,64,256]{3,2,1,0:T(8,128)S(1)} %get-tuple-element.4.field_any, f32[9,64]{1,0:T(8,128)S(1)} %get-tuple-element.5.sums_any), custom_call_target="tpu_custom_call" | custom-call | tf_op jit(solution)/shard_map/pallas_call | solution.py:618
